TPU v7x, 256 devices: a whole 4x4x8 slice. The times are simulated.
256 devices in a mesh: wide: 64 (over x, y_hi, z), narrow: 4 (over y_lo, core).
Axes of the slice: x: 4, y: 4 (y_hi: 2, y_lo: 2; y = y_hi * 2 + y_lo), z: 8, core: 2. Of those that a mesh axis runs over, the one named last changes fastest.
Arguments:
- tokens: bfloat16 [8192, 2048], P('wide'), may hold values from -6 to 6
- expert_ids: int32 [8192, 6], P('wide'), may hold values from 0 to 63, all different within a row; in each aligned block of 128 rows (0 to 127, 128 to 255, ...) at most 16 rows name the same one
- gate_weights: float32 [8192, 6], P('wide'), may hold values from 0.05 to 0.6
- shared_gate: bfloat16 [2048, 2816], P('wide', 'narrow'), may hold values from -0.125 to 0.125
- shared_up: bfloat16 [2048, 2816], P('wide', 'narrow'), may hold values from -0.125 to 0.125
- shared_down: bfloat16 [2816, 2048], P('narrow', 'wide'), may hold values from -0.109375 to 0.109375
- expert_gate: bfloat16 [64, 2048, 1408], P('wide', None, 'narrow'), may hold values from -0.125 to 0.125
- expert_up: bfloat16 [64, 2048, 1408], P('wide', None, 'narrow'), may hold values from -0.125 to 0.125
- expert_down: bfloat16 [64, 1408, 2048], P('wide', 'narrow'), may hold values from -0.15625 to 0.15625
Outputs:
- moe_out: bfloat16 [8192, 2048], P('wide', 'narrow')
Inputs may be any that keep to these rules, and one draw needn't show every extreme that they name: `expert_ids`: the 6 ids of a row differ. Among the 128 rows of one index of wide, no expert is named by more than 16 rows.
All inputs are finite; a program needn't handle non-finite values.
Results may differ from a plain program's by a relative error of at most 0.0075.
Values may be sent and summed in bfloat16 or wider, within the bound.
No kernel may reach another device: no remote copies, remote signals or barrier semaphores. Data moves between devices by JAX's collectives and lax.ppermute only.
A program may use at most 128 MiB of HBM per device.

v0:
```python
import jax
import jax.numpy as jnp
from jax import lax
from jax.experimental import pallas as pl
from jax.experimental.pallas import tpu as pltpu
from jax.sharding import PartitionSpec as P


F32 = jnp.float32
BF16 = jnp.bfloat16
CAP = 16
EXPERTS = 64
SLOTS = EXPERTS * CAP
TOK = 128
D = 2048
FS = 2816
NX = 4
NY = 2
NZ = 8
PAIRS = NZ // 2
CORE_SWAP = [(0, 1), (1, 0), (2, 3), (3, 2)]
Y_SWAP = [(0, 2), (2, 0), (1, 3), (3, 1)]
BOTH_SWAP = [(0, 3), (3, 0), (1, 2), (2, 1)]
COLS = D // 4
CHUNKS = 2
CHUNK_ROWS = SLOTS // CHUNKS
STEP_ROWS = 256
NO_SLOT = 100.0


def moved(dx, flip, dz, pair=0):
    def index(x, y, z):
        return (x % NX * NY + y) * NZ + z % NZ

    return [
        (index(x, y, z), index(x + dx, y ^ flip, (z ^ pair) + dz))
        for x in range(NX)
        for y in range(NY)
        for z in range(NZ)
    ]


def turned_about(k):
    def index(x, y, z, n):
        return ((x * NY + y) * NZ + z) * 4 + n

    return [
        (index(x, y, z, n), index((n + k) % 4, y, z, x))
        for x in range(NX)
        for y in range(NY)
        for z in range(NZ)
        for n in range(4)
    ]


def silu(v):
    return v / (1.0 + jnp.exp(-v))


def dot(a, b):
    return lax.dot_general(a, b, (((1,), (0,)), ((), ())), preferred_element_type=F32)


def dot_nt(a, b):
    return lax.dot_general(a, b, (((1,), (1,)), ((), ())), preferred_element_type=F32)


def named_counts(ids, shape, k_axis):
    expert = lax.broadcasted_iota(jnp.int32, shape, k_axis).astype(F32)
    named = jnp.zeros(shape, F32)
    for k in range(ids.shape[k_axis]):
        one = ids[:, k : k + 1] if k_axis else ids[k : k + 1, :]
        named = named + jnp.where(one == expert, 1.0, 0.0)
    return named


def order_matrix(upper):
    row = lax.broadcasted_iota(jnp.int32, (TOK, TOK), 0)
    col = lax.broadcasted_iota(jnp.int32, (TOK, TOK), 1)
    before = row < col if upper else col < row
    return jnp.where(before, 1.0, 0.0).astype(BF16)


def dispatch_kernel(pos_ref, ids_ref, tok_ref, out_ref):
    del pos_ref
    rows = out_ref.shape[0]
    first = pl.program_id(0) * rows
    named = named_counts(ids_ref[...].astype(F32), (EXPERTS, TOK), 0)
    place = dot(named.astype(BF16), order_matrix(True))
    keys = jnp.where(named > 0.0, place, NO_SLOT).astype(BF16)
    r = lax.broadcasted_iota(jnp.int32, (rows, EXPERTS), 0) + first
    e = lax.broadcasted_iota(jnp.int32, (rows, EXPERTS), 1)
    spread = jnp.where((r >> 4) == e, 1.0, 0.0).astype(BF16)
    wanted = dot(spread, keys)
    slot = ((lax.broadcasted_iota(jnp.int32, (rows, TOK), 0) + first) & 15).astype(F32)
    pick = jnp.where(wanted == slot, 1.0, 0.0).astype(BF16)
    out_ref[...] = dot(pick, tok_ref[...]).astype(BF16)


def dispatch(pos, ids_t, tokens):
    blocks = 2
    rows = SLOTS // blocks
    return pl.pallas_call(
        dispatch_kernel,
        grid_spec=pltpu.PrefetchScalarGridSpec(
            num_scalar_prefetch=1,
            grid=(blocks,),
            in_specs=[
                pl.BlockSpec(ids_t.shape, lambda i, p: (0, 0)),
                pl.BlockSpec((TOK, COLS), lambda i, p: (0, p[0])),
            ],
            out_specs=pl.BlockSpec((rows, COLS), lambda i, p: (i, 0)),
        ),
        out_shape=jax.ShapeDtypeStruct((SLOTS, COLS), BF16),
        name="dispatch",
    )(pos, ids_t, tokens)


def padded_to(value, lanes):
    return jnp.concatenate([value, jnp.zeros((value.shape[0], lanes - value.shape[1]), F32)], axis=1)


def pack_kernel(gate_ref, up_ref, down_ref, out_ref):
    fs = gate_ref.shape[1] // NX
    inward, outward = lanes_of(fs)
    for i in range(NX):
        cut = slice(i * fs, (i + 1) * fs)
        both = jnp.concatenate([gate_ref[:, cut], up_ref[:, cut]], axis=1).astype(F32)
        out_ref[i, :, :inward] = padded_to(both, inward).astype(BF16)
        out_ref[i, :, inward:] = padded_to(down_ref[:, cut].astype(F32), outward).astype(BF16)


def lanes_of(fs):
    return -(-2 * fs // 128) * 128, -(-fs // 128) * 128


def pack(gate, up, down_t):
    return pl.pallas_call(
        pack_kernel,
        out_shape=jax.ShapeDtypeStruct((NX, gate.shape[0], sum(lanes_of(gate.shape[1] // NX))), BF16),
        name="pack",
    )(gate, up, down_t)


def deal_kernel(place_ref, *refs):
    raws, outs = refs[:4], refs[4:]
    n, x, y, z = place_ref[0], place_ref[1], place_ref[2], place_ref[3]
    rows = raws[0].shape[1]
    inward = outs[0].shape[1]
    for i, raw in enumerate(raws):
        at = ((y ^ (i & 1)) * 2 + ((z & 1) ^ (i >> 1))) * rows
        to = pl.ds(pl.multiple_of(at, rows), rows)
        for d in range(NX):
            outs[d][to, :] = raw[pl.ds((x + d) & 3, 1), :, :inward].reshape(rows, inward)
            outs[NX + d][to, :] = raw[pl.ds((n + d) & 3, 1), :, inward:].reshape(
                rows, raw.shape[2] - inward
            )


def deal(place, raws, fs):
    inward, outward = lanes_of(fs)
    rows = 4 * raws[0].shape[1]
    vmem = pl.BlockSpec(memory_space=pltpu.VMEM)
    return pl.pallas_call(
        deal_kernel,
        in_specs=[pl.BlockSpec(memory_space=pltpu.SMEM)] + [vmem] * 4,
        out_specs=[vmem] * 8,
        out_shape=[jax.ShapeDtypeStruct((rows, inward), BF16)] * 4
        + [jax.ShapeDtypeStruct((rows, outward), BF16)] * 4,
        name="deal",
    )(place, *raws)


def stack_kernel(place_ref, *refs):
    pieces, outs = refs[:8], refs[8:]
    x = place_ref[1]
    for d in range(NX):
        at = pl.ds((x - d) & 3, 1)
        outs[0][at] = pieces[d][...][None]
        outs[1][at] = pieces[NX + d][...][None]


def stack(place, pieces):
    vmem = pl.BlockSpec(memory_space=pltpu.VMEM)
    return pl.pallas_call(
        stack_kernel,
        in_specs=[pl.BlockSpec(memory_space=pltpu.SMEM)] + [vmem] * 8,
        out_specs=[vmem] * 2,
        out_shape=[jax.ShapeDtypeStruct((NX,) + pieces[i].shape, BF16) for i in (0, NX)],
        name="stack",
    )(place, *pieces)


def cut_kernel(pos_ref, a, b, c, out_a, out_b, out_c):
    del pos_ref
    out_a[...] = a[0]
    out_b[...] = b[0]
    out_c[...] = c[0]


def cut(pos, w_down):
    mf = w_down.shape[1]
    return pl.pallas_call(
        cut_kernel,
        grid_spec=pltpu.PrefetchScalarGridSpec(
            num_scalar_prefetch=1,
            grid=(1,),
            in_specs=[
                pl.BlockSpec((1, mf, COLS), lambda i, p: (0, 0, p[0] ^ 2)),
                pl.BlockSpec((1, mf, COLS), lambda i, p: (0, 0, p[0] ^ 3)),
                pl.BlockSpec((1, mf, COLS), lambda i, p: (0, 0, p[0] ^ 1)),
            ],
            out_specs=[pl.BlockSpec((mf, COLS), lambda i, p: (0, 0))] * 3,
        ),
        out_shape=[jax.ShapeDtypeStruct((mf, COLS), BF16)] * 3,
        name="cut",
    )(pos, w_down, w_down, w_down)


def hidden_kernel(pos_ref, x0, x1, x2, x3, g0, g1, g2, g3, u0, u1, u2, u3, out_ref):
    del pos_ref
    gate = jnp.zeros((x0.shape[0], g0.shape[1]), F32)
    up = gate
    for x, g, u in ((x0, g0, u0), (x1, g1, u1), (x2, g2, u2), (x3, g3, u3)):
        rows = x[...]
        gate = gate + dot_nt(rows, g[0])
        up = up + dot_nt(rows, u[0])
    mf = gate.shape[1]
    out_ref[:, :mf] = (silu(gate) * up).astype(BF16)
    out_ref[:, mf:] = jnp.zeros((gate.shape[0], out_ref.shape[1] - mf), BF16)


def expert_hidden(pos, chunk, own, core, y, both, w_gate, w_up):
    steps = CHUNK_ROWS // STEP_ROWS
    mf = w_gate.shape[1]
    padded = -(-mf // 128) * 128
    whole = pl.BlockSpec((STEP_ROWS, COLS), lambda i, p: (chunk * steps + i, 0))
    part = pl.BlockSpec((STEP_ROWS, COLS), lambda i, p: (i, 0))
    w_specs = [
        pl.BlockSpec((1, mf, COLS), lambda i, p: (0, 0, p[0])),
        pl.BlockSpec((1, mf, COLS), lambda i, p: (0, 0, p[0] ^ 1)),
        pl.BlockSpec((1, mf, COLS), lambda i, p: (0, 0, p[0] ^ 2)),
        pl.BlockSpec((1, mf, COLS), lambda i, p: (0, 0, p[0] ^ 3)),
    ]
    return pl.pallas_call(
        hidden_kernel,
        grid_spec=pltpu.PrefetchScalarGridSpec(
            num_scalar_prefetch=1,
            grid=(steps,),
            in_specs=[whole, whole, part, part] + w_specs + w_specs,
            out_specs=pl.BlockSpec((STEP_ROWS, padded), lambda i, p: (i, 0)),
        ),
        out_shape=jax.ShapeDtypeStruct((CHUNK_ROWS, padded), BF16),
        cost_estimate=pl.CostEstimate(
            flops=4 * CHUNK_ROWS * D * mf, bytes_accessed=6_000_000, transcendentals=CHUNK_ROWS * mf
        ),
        name="hidden",
    )(pos, own, core, y, both, *[w_gate] * 4, *[w_up] * 4)


def down_kernel(pos_ref, h0, h1, h2, h3, w0, w1, w2, w3, *rest):
    del pos_ref
    out_ref = rest[-1]
    mf = w1.shape[0]
    total = dot(h0[:, :mf], w0[0])
    for h, w in ((h1, w1), (h2, w2), (h3, w3)):
        total = total + dot(h[:, :mf], w[...])
    out_ref[...] = total.astype(BF16)


def expert_columns(pos, chunk, hiddens, w_own, w_others, so_far):
    steps = CHUNK_ROWS // STEP_ROWS
    mf = w_own.shape[1]
    h_spec = pl.BlockSpec((STEP_ROWS, hiddens[0].shape[1]), lambda i, p: (i, 0))
    w_spec = pl.BlockSpec((mf, COLS), lambda i, p: (0, 0))
    more = [] if so_far is None else [so_far]
    return pl.pallas_call(
        down_kernel,
        grid_spec=pltpu.PrefetchScalarGridSpec(
            num_scalar_prefetch=1,
            grid=(steps,),
            in_specs=[h_spec] * 4
            + [pl.BlockSpec((1, mf, COLS), lambda i, p: (0, 0, p[0]))]
            + [w_spec] * 3
            + [pl.BlockSpec(memory_space=pl.ANY)] * len(more),
            out_specs=pl.BlockSpec((STEP_ROWS, COLS), lambda i, p: (chunk * steps + i, 0)),
        ),
        out_shape=jax.ShapeDtypeStruct((SLOTS, COLS), BF16),
        input_output_aliases={9: 0} if more else {},
        cost_estimate=pl.CostEstimate(
            flops=8 * CHUNK_ROWS * COLS * mf, bytes_accessed=4_000_000, transcendentals=0
        ),
        name="down",
    )(pos, *hiddens, w_own, *w_others, *more)


def fetch(blocks, w_ref, sems, z):
    copies = []
    for step, block in enumerate(blocks):
        to = w_ref.at[((z >> 1) - step) & (PAIRS - 1)]
        copies.append(pltpu.make_async_copy(block, to, sems.at[step]))
    for copy in copies:
        copy.start()
    for copy in copies:
        copy.wait()


def shared_hidden_kernel(place_ref, t0, t1, t2, t3, *refs):
    blocks, (out_ref, w_ref, sems) = refs[:PAIRS], refs[PAIRS + 1 :]
    z = place_ref[3]
    fetch(blocks, w_ref, sems, z)
    rows = PAIRS * w_ref.shape[3]
    lanes = w_ref.shape[4]
    fs = FS // (4 * NX)
    total = jnp.zeros((NX * TOK, lanes), F32)
    for quarter in range(NX):
        for half in range(NY):
            w = w_ref[:, quarter, half].reshape(rows, lanes)
            first = (quarter * NY + half) * rows
            tok = jnp.concatenate([t[:, first : first + rows] for t in (t0, t1, t2, t3)], axis=0)
            total = total + dot(tok, w)
    hidden = silu(total[:, :fs]) * total[:, fs : 2 * fs]
    out_ref[...] = padded_to(hidden, out_ref.shape[1]).astype(BF16)


def shared_hidden(place, toks, blocks, after, units):
    lanes = blocks[0].shape[3]
    vmem = pl.BlockSpec(memory_space=pltpu.VMEM)
    return pl.pallas_call(
        shared_hidden_kernel,
        in_specs=[pl.BlockSpec(memory_space=pltpu.SMEM)]
        + [vmem] * 4
        + [pl.BlockSpec(memory_space=pl.ANY)] * (PAIRS + 1),
        out_specs=vmem,
        out_shape=jax.ShapeDtypeStruct((NX * TOK, units), BF16),
        scratch_shapes=[
            pltpu.VMEM((PAIRS,) + blocks[0].shape, BF16),
            pltpu.SemaphoreType.DMA((PAIRS,)),
        ],
        cost_estimate=pl.CostEstimate(
            flops=2 * NX * TOK * D * lanes, bytes_accessed=5_000_000, transcendentals=NX * TOK * units
        ),
        name="shared_hidden",
    )(place, *toks, *blocks, after)


def shared_down_kernel(place_ref, h0, h1, h2, h3, *refs):
    blocks, outs, (w_ref, sems) = refs[:PAIRS], refs[PAIRS + 1 : PAIRS + 5], refs[PAIRS + 5 :]
    n, z = place_ref[0], place_ref[3]
    units = w_ref.shape[4]
    fetch(blocks, w_ref, sems, z)
    rows = PAIRS * w_ref.shape[3]
    for half in range(NY):
        total = jnp.zeros((NX * TOK, rows), F32)
        for j, h in enumerate((h0, h1, h2, h3)):
            w = w_ref[:, pl.ds(n ^ j, 1), half].reshape(rows, units)
            total = total + dot_nt(h[...], w)
        for d in range(NX):
            outs[d][:, half * rows : (half + 1) * rows] = total[d * TOK : (d + 1) * TOK].astype(BF16)


def shared_columns(place, hiddens, blocks, after):
    vmem = pl.BlockSpec(memory_space=pltpu.VMEM)
    units = hiddens[0].shape[1]
    return pl.pallas_call(
        shared_down_kernel,
        in_specs=[pl.BlockSpec(memory_space=pltpu.SMEM)]
        + [vmem] * 4
        + [pl.BlockSpec(memory_space=pl.ANY)] * (PAIRS + 1),
        out_specs=[vmem] * 4,
        out_shape=[jax.ShapeDtypeStruct((TOK, COLS), BF16)] * 4,
        scratch_shapes=[
            pltpu.VMEM((PAIRS,) + blocks[0].shape, BF16),
            pltpu.SemaphoreType.DMA((PAIRS,)),
        ],
        cost_estimate=pl.CostEstimate(
            flops=2 * NX * TOK * D * units, bytes_accessed=4_000_000, transcendentals=0
        ),
        name="shared_down",
    )(place, *hiddens, *blocks, after)


def turned(values):
    row = lax.broadcasted_iota(jnp.int32, (TOK, TOK), 0)
    col = lax.broadcasted_iota(jnp.int32, (TOK, TOK), 1)
    eye = jnp.where(row == col, 1.0, 0.0).astype(BF16)
    total = None
    rest = values
    for _ in range(3):
        part = rest.astype(BF16)
        rest = rest - part.astype(F32)
        moved = dot_nt(eye, part)
        total = moved if total is None else total + moved
    return total


def combine_kernel(ids_ref, gw_ref, ret_ref, s0, s1, s2, s3, out_ref):
    ids = turned(ids_ref[...].astype(F32))
    gates = turned(gw_ref[...])
    named = named_counts(ids, (TOK, EXPERTS), 1)
    place = dot(order_matrix(False), named.astype(BF16))
    keys = jnp.where(named > 0.0, place, NO_SLOT).astype(BF16)
    lane = lax.broadcasted_iota(jnp.int32, (TOK, EXPERTS), 1).astype(F32)
    weight = jnp.zeros((TOK, EXPERTS), F32)
    for k in range(ids.shape[1]):
        weight = weight + jnp.where(ids[:, k : k + 1] == lane, gates[:, k : k + 1], 0.0)
    e = lax.broadcasted_iota(jnp.int32, (EXPERTS, SLOTS), 0)
    r = lax.broadcasted_iota(jnp.int32, (EXPERTS, SLOTS), 1)
    spread = jnp.where((r >> 4) == e, 1.0, 0.0).astype(BF16)
    slot = (lax.broadcasted_iota(jnp.int32, (TOK, SLOTS), 1) & 15).astype(F32)
    hit = dot(keys, spread) == slot
    ret = ret_ref[...]
    total = s0[...].astype(F32)
    for part in (s1, s2, s3):
        total = total + part[...].astype(F32)
    rest = weight
    for _ in range(3):
        part = rest.astype(BF16)
        rest = rest - part.astype(F32)
        row = jnp.where(hit, dot(part, spread), 0.0).astype(BF16)
        total = total + dot(row, ret)
    out_ref[...] = total.astype(BF16)


def combine(ids, gate_weights, returned, shared):
    return pl.pallas_call(
        combine_kernel,
        out_shape=jax.ShapeDtypeStruct((TOK, COLS), BF16),
        name="combine",
    )(ids, gate_weights, returned, *shared)


def body(
    tokens,
    expert_ids,
    gate_weights,
    shared_gate,
    shared_up,
    shared_down,
    expert_gate,
    expert_up,
    expert_down,
):
    pos = lax.axis_index("narrow").astype(jnp.int32).reshape(1)
    ids_t = expert_ids.T
    gates_t = gate_weights.T
    gate_t = expert_gate.transpose(0, 2, 1)
    up_t = expert_up.transpose(0, 2, 1)

    wide = lax.axis_index("wide").astype(jnp.int32)
    place = jnp.stack([pos[0], wide >> 4, (wide >> 3) & 1, wide & 7])

    raw = pack(shared_gate, shared_up, shared_down.T)
    raws = [raw] + [lax.ppermute(raw, "wide", moved(0, i & 1, 0, i >> 1)) for i in (1, 2, 3)]

    outgoing = dispatch(pos, ids_t, tokens).reshape(EXPERTS, CAP, COLS)
    own = lax.all_to_all(outgoing, "wide", 0, 0, tiled=True).reshape(SLOTS, COLS)

    pieces = list(deal(place, raws, shared_gate.shape[1] // NX))
    for d in range(NX):
        pieces[NX + d] = lax.ppermute(pieces[NX + d], ("wide", "narrow"), turned_about(d))
    for d in range(1, NX):
        pieces[d] = lax.ppermute(pieces[d], "wide", moved(d, 0, 0))
    cuts = cut(pos, expert_down)
    others = [
        lax.ppermute(w, "narrow", swap)
        for w, swap in zip(cuts, (Y_SWAP, BOTH_SWAP, CORE_SWAP))
    ]
    columns = stack(place, pieces)
    inward, outward = [
        [c.reshape(NX, NY, c.shape[1] // NY, c.shape[2])] for c in columns
    ]
    for blocks in (inward, outward):
        for k in range(1, PAIRS):
            blocks.append(lax.ppermute(blocks[0], "wide", moved(0, 0, 2 * k)))
    toks = [tokens]
    for d in range(1, NX):
        toks.append(lax.ppermute(tokens, "wide", moved(d, 0, 0)))

    ys = []
    for k in range(CHUNKS):
        ys.append(lax.ppermute(own[k * CHUNK_ROWS : (k + 1) * CHUNK_ROWS], "narrow", Y_SWAP))
    core = lax.ppermute(own, "narrow", CORE_SWAP)
    hiddens = []
    for k in range(CHUNKS):
        both = lax.ppermute(ys[k], "narrow", CORE_SWAP)
        hidden = expert_hidden(pos, k, own, core, ys[k], both, gate_t, up_t)
        hidden_y = lax.ppermute(hidden, "narrow", Y_SWAP)
        hidden_core = lax.ppermute(hidden, "narrow", CORE_SWAP)
        hiddens.append([hidden, hidden_y, hidden_core])
    common = shared_hidden(place, toks, inward, hiddens[-1][0], pieces[NX].shape[1])
    common_y = lax.ppermute(common, "narrow", Y_SWAP)
    common_core = lax.ppermute(common, "narrow", CORE_SWAP)
    common_both = lax.ppermute(common_y, "narrow", CORE_SWAP)
    outputs = None
    for k in range(CHUNKS):
        hidden_both = lax.ppermute(hiddens[k][1], "narrow", CORE_SWAP)
        hiddens[k].insert(2, hidden_both)
        outputs = expert_columns(pos, k, hiddens[k], expert_down, others, outputs)
    returned = lax.all_to_all(outputs.reshape(EXPERTS, CAP, COLS), "wide", 0, 0, tiled=True)

    shared = list(shared_columns(place, [common, common_core, common_y, common_both], outward, outputs))
    for d in range(1, NX):
        shared[d] = lax.ppermute(shared[d], "wide", moved(-d, 0, 0))
    return combine(ids_t, gates_t, returned.reshape(SLOTS, COLS), shared)


def solution(mesh):
    in_specs = (
        P("wide", None),
        P("wide", None),
        P("wide", None),
        P("wide", "narrow"),
        P("wide", "narrow"),
        P("narrow", "wide"),
        P("wide", None, "narrow"),
        P("wide", None, "narrow"),
        P("wide", "narrow", None),
    )
    out_specs = P("wide", "narrow")
    return jax.shard_map(body, mesh=mesh, in_specs=in_specs, out_specs=out_specs, check_vma=False)
```

profile of v0, /device:TPU:1, one launch (start us, length us, event | category | flops | bytes accessed | tf_op | source)
XLA Modules:
  0.0 307.1 jit_solution(4300522309032186047)
XLA Ops:
  2.8 42.4 %all_to_all.10 = bf16[64,16,512]{2,1,0:T(8,128)(2,1)S(1)} all-to-all(bf16[64,16,512]{2,1,0:T(8,128)(2,1)} %bitcast.38), channel_id=1, replica_groups=mesh['wide'=64,'narrow'=4] {'wide'}, dimensions={0} | all-to-all | bytes 2097152 | tf_op jit(solution)/shard_map/all_to_all | solution.py:457
  45.2 4.2 %collective-permute-start = (bf16[1024,512]{1,0:T(8,128)(2,1)S(1)}, bf16[1024,512]{1,0:T(8,128)(2,1)S(1)}, u32[]{:S(2)}, u32[]{:S(2)}) collective-permute-start(bf16[1024,512]{1,0:T(8,128)(2,1)S(1)} %bitcast.33), channel_id=1, source_target_pairs={{0,1},{1,0},{2,3},{3,2},{4,5},{5,4},{6,7},{7,6},{8,9},{9,8},{10,11... | collective-permute-start | bytes 3145736 | tf_op jit(solution)/shard_map/ppermute | solution.py:483
  51.0 12.0 %collective-permute-done.9.x2 = bf16[512,512]{1,0:T(8,128)(2,1)S(1)} collective-permute-done((bf16[512,512]{1,0:T(8,128)(2,1)S(1)}, bf16[512,512]{1,0:T(8,128)(2,1)S(1)}, u32[]{:S(2)}, u32[]{:S(2)}) %collective-permute-start.9) | collective-permute-done | bytes 524320 | tf_op jit(solution)/shard_map/ppermute | solution.py:482
  64.4 10.0 %collective-permute-done.1.x2 = bf16[512,512]{1,0:T(8,128)(2,1)} collective-permute-done((bf16[512,512]{1,0:T(8,128)(2,1)S(1)}, bf16[512,512]{1,0:T(8,128)(2,1)}, u32[]{:S(2)}, u32[]{:S(2)}) %collective-permute-start.1) | collective-permute-done | bytes 524320 | tf_op jit(solution)/shard_map/ppermute | solution.py:482
  78.9 5.4 %hidden.3.h0 = bf16[512,384]{1,0:T(8,128)(2,1)} custom-call(s32[1]{0:T(128)} %bitcast.2.pos_ref, bf16[1024,512]{1,0:T(8,128)(2,1)} %bitcast.34, bf16[1024,512]{1,0:T(8,128)(2,1)} %copy-done.1, bf16[512,512]{1,0:T(8,128)(2,1)} %copy-done.11, bf16[512,512]{1,0:T(8,128)(2,1)} %collective-permute-done.10.x3, bf16[1,352,2048]{2,1,0:T(8,128)(2,1)} %bitcast.17, ...), custom_call_target="tpu_custom_call" | custom-call | flops 1476395008 | bytes 6000000 | tf_op jit(solution)/shard_map/hidden/pallas_call | solution.py:245
  85.5 5.5 %hidden.2.h0.refs_4_ = bf16[512,384]{1,0:T(8,128)(2,1)} custom-call(s32[1]{0:T(128)} %bitcast.2.pos_ref, bf16[1024,512]{1,0:T(8,128)(2,1)} %bitcast.35, bf16[1024,512]{1,0:T(8,128)(2,1)} %copy-done.1, bf16[512,512]{1,0:T(8,128)(2,1)} %collective-permute-done.1.x2, bf16[512,512]{1,0:T(8,128)(2,1)} %collective-permute-done.2.x3, ...), custom_call_target="tpu_custom_call" | custom-call | flops 1476395008 | bytes 6000000 | tf_op jit(solution)/shard_map/hidden/pallas_call | solution.py:245
  97.5 14.9 %collective-permute-done.7.w2 = bf16[352,512]{1,0:T(8,128)(2,1)S(1)} collective-permute-done((bf16[352,512]{1,0:T(8,128)(2,1)S(1)}, bf16[352,512]{1,0:T(8,128)(2,1)S(1)}, u32[]{:S(2)}, u32[]{:S(2)}) %collective-permute-start.7) | collective-permute-done | bytes 360480 | tf_op jit(solution)/shard_map/ppermute | solution.py:466
  113.8 3.9 %down.2.rest_0_ = bf16[1024,512]{1,0:T(8,128)(2,1)} custom-call(s32[1]{0:T(128)} %bitcast.2.pos_ref, bf16[512,384]{1,0:T(8,128)(2,1)} %hidden.3.h0, bf16[512,384]{1,0:T(8,128)(2,1)} %copy-done.16, bf16[512,384]{1,0:T(8,128)(2,1)} %collective-permute-done.12.h2, bf16[512,384]{1,0:T(8,128)(2,1)} %copy-done.17, bf16[1,352,2048]{2,1,0:T(8,128)(2,1)} %w0.3, ...), custom_call_target="tpu_custom_call" | custom-call | flops 738197504 | bytes 4000000 | tf_op jit(solution)/shard_map/down/pallas_call | solution.py:277
  119.3 3.9 %down.3.refs_4_ = bf16[1024,512]{1,0:T(8,128)(2,1)} custom-call(s32[1]{0:T(128)} %bitcast.2.pos_ref, bf16[512,384]{1,0:T(8,128)(2,1)} %hidden.2.h0.refs_4_, bf16[512,384]{1,0:T(8,128)(2,1)} %copy-done.12, bf16[512,384]{1,0:T(8,128)(2,1)} %copy-done.15, bf16[512,384]{1,0:T(8,128)(2,1)} %copy-done.13, ...), custom_call_target="tpu_custom_call", output_to_operand_aliasing={{}: (9, {})} | custom-call | flops 738197504 | bytes 4000000 | tf_op jit(solution)/shard_map/down/pallas_call | solution.py:277
  123.2 6.1 %all-to-all-start.1 = ((bf16[64,16,512]{2,1,0:T(8,128)(2,1)}), bf16[64,16,512]{2,1,0:T(8,128)(2,1)S(1)}, u32[]{:S(2)}, u32[]{:S(2)}) async-start(bf16[64,16,512]{2,1,0:T(8,128)(2,1)} %bitcast.36), calls=%async_computation.1 | async-start | bytes 2097152 | tf_op jit(solution)/shard_map/all_to_all | solution.py:500
  136.7 5.2 %collective-permute-done.17.refs_1_ = bf16[4,32,640]{2,1,0:T(8,128)(2,1)S(1)} collective-permute-done((bf16[4,32,640]{2,1,0:T(8,128)(2,1)}, bf16[4,32,640]{2,1,0:T(8,128)(2,1)S(1)}, u32[]{:S(2)}, u32[]{:S(2)}) %collective-permute-start.17) | collective-permute-done | bytes 163872 | tf_op jit(solution)/shard_map/ppermute | solution.py:454
  141.9 14.5 %collective-permute-done.18.refs_2_ = bf16[4,32,640]{2,1,0:T(8,128)(2,1)S(1)} collective-permute-done((bf16[4,32,640]{2,1,0:T(8,128)(2,1)}, bf16[4,32,640]{2,1,0:T(8,128)(2,1)S(1)}, u32[]{:S(2)}, u32[]{:S(2)}) %collective-permute-start.18) | collective-permute-done | bytes 163872 | tf_op jit(solution)/shard_map/ppermute | solution.py:454
  156.4 5.9 %collective-permute-done.19.refs_3_ = bf16[4,32,640]{2,1,0:T(8,128)(2,1)S(1)} collective-permute-done((bf16[4,32,640]{2,1,0:T(8,128)(2,1)}, bf16[4,32,640]{2,1,0:T(8,128)(2,1)S(1)}, u32[]{:S(2)}, u32[]{:S(2)}) %collective-permute-start.19) | collective-permute-done | bytes 163872 | tf_op jit(solution)/shard_map/ppermute | solution.py:454
  165.1 4.3 %collective-permute-start.23 = (bf16[128,256]{1,0:T(8,128)(2,1)}, bf16[128,256]{1,0:T(8,128)(2,1)S(1)}, u32[]{:S(2)}, u32[]{:S(2)}) collective-permute-start(bf16[128,256]{1,0:T(8,128)(2,1)} %get-tuple-element.29), channel_id=1, source_target_pairs={{0,0},{1,64},{2,128},{3,192},{4,4},{5,68},{6,132},{7,196},{8,8},{9... | collective-permute-start | bytes 196616 | tf_op jit(solution)/shard_map/ppermute | solution.py:461
  174.6 4.1 %collective-permute-start.15 = (bf16[128,2048]{1,0:T(8,128)(2,1)S(1)}, bf16[128,2048]{1,0:T(8,128)(2,1)S(1)}, u32[]{:S(2)}, u32[]{:S(2)}) collective-permute-start(bf16[128,2048]{1,0:T(8,128)(2,1)S(1)} %copy-done.3), channel_id=1, source_target_pairs={{0,128},{4,132},{8,136},{12,140},{16,144},{20,148},{24,152},{28,15... | collective-permute-start | bytes 1572872 | tf_op jit(solution)/shard_map/ppermute | solution.py:478
  182.7 11.8 %collective-permute-done.21.refs_2_ = bf16[128,384]{1,0:T(8,128)(2,1)S(1)} collective-permute-done((bf16[128,384]{1,0:T(8,128)(2,1)}, bf16[128,384]{1,0:T(8,128)(2,1)S(1)}, u32[]{:S(2)}, u32[]{:S(2)}) %collective-permute-start.21) | collective-permute-done | bytes 98336 | tf_op jit(solution)/shard_map/ppermute | solution.py:463
  194.5 12.3 %collective-permute-done.22.refs_3_ = bf16[128,384]{1,0:T(8,128)(2,1)S(1)} collective-permute-done((bf16[128,384]{1,0:T(8,128)(2,1)}, bf16[128,384]{1,0:T(8,128)(2,1)S(1)}, u32[]{:S(2)}, u32[]{:S(2)}) %collective-permute-start.22) | collective-permute-done | bytes 98336 | tf_op jit(solution)/shard_map/ppermute | solution.py:463
  217.3 7.3 %collective-permute-done.27.refs_1_ = bf16[4,2,64,384]{3,2,1,0:T(8,128)(2,1)S(1)} collective-permute-done((bf16[4,2,64,384]{3,2,1,0:T(8,128)(2,1)}, bf16[4,2,64,384]{3,2,1,0:T(8,128)(2,1)S(1)}, u32[]{:S(2)}, u32[]{:S(2)}) %collective-permute-start.27) | collective-permute-done | bytes 393248 | tf_op jit(solution)/shard_map/ppermute | solution.py:475
  224.6 14.2 %collective-permute-done.28.refs_2_ = bf16[4,2,64,384]{3,2,1,0:T(8,128)(2,1)} collective-permute-done((bf16[4,2,64,384]{3,2,1,0:T(8,128)(2,1)}, bf16[4,2,64,384]{3,2,1,0:T(8,128)(2,1)}, u32[]{:S(2)}, u32[]{:S(2)}) %collective-permute-start.28) | collective-permute-done | bytes 393248 | tf_op jit(solution)/shard_map/ppermute | solution.py:475
  238.8 11.5 %collective-permute-done.29.refs_3_ = bf16[4,2,64,384]{3,2,1,0:T(8,128)(2,1)} collective-permute-done((bf16[4,2,64,384]{3,2,1,0:T(8,128)(2,1)}, bf16[4,2,64,384]{3,2,1,0:T(8,128)(2,1)}, u32[]{:S(2)}, u32[]{:S(2)}) %collective-permute-start.29) | collective-permute-done | bytes 393248 | tf_op jit(solution)/shard_map/ppermute | solution.py:475
  250.3 5.0 %shared_hidden.1.h0 = bf16[512,256]{1,0:T(8,128)(2,1)} custom-call(s32[4]{0:T(128)} %pad_add_fusion.place_ref, bf16[128,2048]{1,0:T(8,128)(2,1)} %t0.1, bf16[128,2048]{1,0:T(8,128)(2,1)} %copy-done.8, bf16[128,2048]{1,0:T(8,128)(2,1)} %copy-done.9, bf16[128,2048]{1,0:T(8,128)(2,1)} %copy-done.10, bf16[4,2,64,384]{3,2,1,0:T(8,128)(2,1)} %bitcast.44, ...), custom_call_target="tpu_custom_call" | custom-call | flops 805306368 | bytes 5000000 | tf_op jit(solution)/shard_map/shared_hidden/pallas_call | solution.py:329
  264.7 5.4 %collective-permute-done.33.refs_1_ = bf16[4,2,64,256]{3,2,1,0:T(8,128)(2,1)S(1)} collective-permute-done((bf16[4,2,64,256]{3,2,1,0:T(8,128)(2,1)}, bf16[4,2,64,256]{3,2,1,0:T(8,128)(2,1)S(1)}, u32[]{:S(2)}, u32[]{:S(2)}) %collective-permute-start.33) | collective-permute-done | bytes 262176 | tf_op jit(solution)/shard_map/ppermute | solution.py:475
  270.1 9.6 %collective-permute-done.34.refs_2_ = bf16[4,2,64,256]{3,2,1,0:T(8,128)(2,1)S(1)} collective-permute-done((bf16[4,2,64,256]{3,2,1,0:T(8,128)(2,1)}, bf16[4,2,64,256]{3,2,1,0:T(8,128)(2,1)S(1)}, u32[]{:S(2)}, u32[]{:S(2)}) %collective-permute-start.34) | collective-permute-done | bytes 262176 | tf_op jit(solution)/shard_map/ppermute | solution.py:475
  288.0 4.6 %collective-permute-start.36 = (bf16[128,512]{1,0:T(8,128)(2,1)}, bf16[128,512]{1,0:T(8,128)(2,1)S(1)}, u32[]{:S(2)}, u32[]{:S(2)}) collective-permute-start(bf16[128,512]{1,0:T(8,128)(2,1)} %get-tuple-element.36), channel_id=1, source_target_pairs={{0,192},{4,196},{8,200},{12,204},{16,208},{20,212},{24,216},{28,22... | collective-permute-start | bytes 393224 | tf_op jit(solution)/shard_map/ppermute | solution.py:504
  (147 shorter events, 82.9 us)
Async XLA Ops:
  45.2 32.7 %collective-permute-start = (bf16[1024,512]{1,0:T(8,128)(2,1)S(1)}, bf16[1024,512]{1,0:T(8,128)(2,1)S(1)}, u32[]{:S(2)}, u32[]{:S(2)}) collective-permute-start(bf16[1024,512]{1,0:T(8,128)(2,1)S(1)} %bitcast.33), channel_id=1, source_target_pairs={{0,1},{1,0},{2,3},{3,2},{4,5},{5,4},{6,7},{7,6},{8,9},{9,8},{10,11... | collective-permute-start | bytes 3145736 | tf_op jit(solution)/shard_map/ppermute | solution.py:483
  50.0 24.4 %collective-permute-start.1 = (bf16[512,512]{1,0:T(8,128)(2,1)S(1)}, bf16[512,512]{1,0:T(8,128)(2,1)}, u32[]{:S(2)}, u32[]{:S(2)}) collective-permute-start(bf16[512,512]{1,0:T(8,128)(2,1)S(1)} %bitcast.39), channel_id=1, source_target_pairs={{0,2},{2,0},{1,3},{3,1},{4,6},{6,4},{5,7},{7,5},{8,10},{10,8},{9,1... | collective-permute-start | bytes 1572872 | tf_op jit(solution)/shard_map/ppermute | solution.py:482
  63.1 14.8 %collective-permute-start.10 = (bf16[512,512]{1,0:T(8,128)(2,1)S(1)}, bf16[512,512]{1,0:T(8,128)(2,1)}, u32[]{:S(2)}, u32[]{:S(2)}) collective-permute-start(bf16[512,512]{1,0:T(8,128)(2,1)S(1)} %collective-permute-done.9.x2), channel_id=1, source_target_pairs={{0,1},{1,0},{2,3},{3,2},{4,5},{5,4},{6,7},{7,6},{8,9},{9,8},{10,11... | collective-permute-start | bytes 1572872 | tf_op jit(solution)/shard_map/ppermute | solution.py:486
  77.5 20.0 %collective-permute-start.6 = (bf16[352,512]{1,0:T(8,128)(2,1)}, bf16[352,512]{1,0:T(8,128)(2,1)S(1)}, u32[]{:S(2)}, u32[]{:S(2)}) collective-permute-start(bf16[352,512]{1,0:T(8,128)(2,1)} %get-tuple-element.22), channel_id=1, source_target_pairs={{0,2},{2,0},{1,3},{3,1},{4,6},{6,4},{5,7},{7,5},{8,10},{10,8},{9,1... | collective-permute-start | bytes 1081352 | tf_op jit(solution)/shard_map/ppermute | solution.py:466
  91.0 21.7 %collective-permute-start.3 = (bf16[512,384]{1,0:T(8,128)(2,1)}, bf16[512,384]{1,0:T(8,128)(2,1)S(1)}, u32[]{:S(2)}, u32[]{:S(2)}) collective-permute-start(bf16[512,384]{1,0:T(8,128)(2,1)} %hidden.2.h0.refs_4_), channel_id=1, source_target_pairs={{0,2},{2,0},{1,3},{3,1},{4,6},{6,4},{5,7},{7,5},{8,10},{10,8},{9,1... | collective-permute-start | bytes 1179656 | tf_op jit(solution)/shard_map/ppermute | solution.py:488
  91.4 21.1 %collective-permute-start.7 = (bf16[352,512]{1,0:T(8,128)(2,1)S(1)}, bf16[352,512]{1,0:T(8,128)(2,1)S(1)}, u32[]{:S(2)}, u32[]{:S(2)}) collective-permute-start(bf16[352,512]{1,0:T(8,128)(2,1)S(1)} %copy-done.37), channel_id=1, source_target_pairs={{0,3},{3,0},{1,2},{2,1},{4,7},{7,4},{5,6},{6,5},{8,11},{11,8},{9,1... | collective-permute-start | bytes 1081352 | tf_op jit(solution)/shard_map/ppermute | solution.py:466
  93.2 19.8 %collective-permute-start.13 = (bf16[512,384]{1,0:T(8,128)(2,1)S(1)}, bf16[512,384]{1,0:T(8,128)(2,1)S(1)}, u32[]{:S(2)}, u32[]{:S(2)}) collective-permute-start(bf16[512,384]{1,0:T(8,128)(2,1)S(1)} %copy-done.4), channel_id=1, source_target_pairs={{0,1},{1,0},{2,3},{3,2},{4,5},{5,4},{6,7},{7,6},{8,9},{9,8},{10,11... | collective-permute-start | bytes 1179656 | tf_op jit(solution)/shard_map/ppermute | solution.py:489
  96.1 17.6 %collective-permute-start.12 = (bf16[512,384]{1,0:T(8,128)(2,1)S(1)}, bf16[512,384]{1,0:T(8,128)(2,1)}, u32[]{:S(2)}, u32[]{:S(2)}) collective-permute-start(bf16[512,384]{1,0:T(8,128)(2,1)S(1)} %collective-permute-done.11.h1), channel_id=1, source_target_pairs={{0,1},{1,0},{2,3},{3,2},{4,5},{5,4},{6,7},{7,6},{8,9},{9,8},{10,11... | collective-permute-start | bytes 1179656 | tf_op jit(solution)/shard_map/ppermute | solution.py:497
  97.4 15.5 %collective-permute-start.8 = (bf16[352,512]{1,0:T(8,128)(2,1)}, bf16[352,512]{1,0:T(8,128)(2,1)S(1)}, u32[]{:S(2)}, u32[]{:S(2)}) collective-permute-start(bf16[352,512]{1,0:T(8,128)(2,1)} %get-tuple-element.24), channel_id=1, source_target_pairs={{0,1},{1,0},{2,3},{3,2},{4,5},{5,4},{6,7},{7,6},{8,9},{9,8},{10,11... | collective-permute-start | bytes 1081352 | tf_op jit(solution)/shard_map/ppermute | solution.py:466
  123.2 179.3 %all-to-all-start.1 = ((bf16[64,16,512]{2,1,0:T(8,128)(2,1)}), bf16[64,16,512]{2,1,0:T(8,128)(2,1)S(1)}, u32[]{:S(2)}, u32[]{:S(2)}) async-start(bf16[64,16,512]{2,1,0:T(8,128)(2,1)} %bitcast.36), calls=%async_computation.1 | async-start | bytes 2097152 | tf_op jit(solution)/shard_map/all_to_all | solution.py:500
  129.3 84.9 %collective-permute-start.14 = (bf16[128,2048]{1,0:T(8,128)(2,1)S(1)}, bf16[128,2048]{1,0:T(8,128)(2,1)S(1)}, u32[]{:S(2)}, u32[]{:S(2)}) collective-permute-start(bf16[128,2048]{1,0:T(8,128)(2,1)S(1)} %copy-done.3), channel_id=1, source_target_pairs={{0,64},{4,68},{8,72},{12,76},{16,80},{20,84},{24,88},{28,92},{32,9... | collective-permute-start | bytes 1572872 | tf_op jit(solution)/shard_map/ppermute | solution.py:478
  134.7 21.7 %collective-permute-start.18 = (bf16[4,32,640]{2,1,0:T(8,128)(2,1)}, bf16[4,32,640]{2,1,0:T(8,128)(2,1)S(1)}, u32[]{:S(2)}, u32[]{:S(2)}) collective-permute-start(bf16[4,32,640]{2,1,0:T(8,128)(2,1)} %pack.1.refs_0_), channel_id=1, source_target_pairs={{0,4},{4,0},{8,12},{12,8},{16,20},{20,16},{24,28},{28,24},{32,36},... | collective-permute-start | bytes 491528 | tf_op jit(solution)/shard_map/ppermute | solution.py:454
  135.9 26.5 %collective-permute-start.19 = (bf16[4,32,640]{2,1,0:T(8,128)(2,1)}, bf16[4,32,640]{2,1,0:T(8,128)(2,1)S(1)}, u32[]{:S(2)}, u32[]{:S(2)}) collective-permute-start(bf16[4,32,640]{2,1,0:T(8,128)(2,1)} %pack.1.refs_0_), channel_id=1, source_target_pairs={{0,36},{4,32},{8,44},{12,40},{16,52},{20,48},{24,60},{28,56},{32,4... | collective-permute-start | bytes 491528 | tf_op jit(solution)/shard_map/ppermute | solution.py:454
  174.6 42.7 %collective-permute-start.15 = (bf16[128,2048]{1,0:T(8,128)(2,1)S(1)}, bf16[128,2048]{1,0:T(8,128)(2,1)S(1)}, u32[]{:S(2)}, u32[]{:S(2)}) collective-permute-start(bf16[128,2048]{1,0:T(8,128)(2,1)S(1)} %copy-done.3), channel_id=1, source_target_pairs={{0,128},{4,132},{8,136},{12,140},{16,144},{20,148},{24,152},{28,15... | collective-permute-start | bytes 1572872 | tf_op jit(solution)/shard_map/ppermute | solution.py:478
  178.7 38.6 %collective-permute-start.16 = (bf16[128,2048]{1,0:T(8,128)(2,1)S(1)}, bf16[128,2048]{1,0:T(8,128)(2,1)S(1)}, u32[]{:S(2)}, u32[]{:S(2)}) collective-permute-start(bf16[128,2048]{1,0:T(8,128)(2,1)S(1)} %copy-done.3), channel_id=1, source_target_pairs={{0,192},{4,196},{8,200},{12,204},{16,208},{20,212},{24,216},{28,22... | collective-permute-start | bytes 1572872 | tf_op jit(solution)/shard_map/ppermute | solution.py:478
  179.3 15.2 %collective-permute-start.21 = (bf16[128,384]{1,0:T(8,128)(2,1)}, bf16[128,384]{1,0:T(8,128)(2,1)S(1)}, u32[]{:S(2)}, u32[]{:S(2)}) collective-permute-start(bf16[128,384]{1,0:T(8,128)(2,1)} %get-tuple-element.27), channel_id=1, source_target_pairs={{0,128},{4,132},{8,136},{12,140},{16,144},{20,148},{24,152},{28,15... | collective-permute-start | bytes 294920 | tf_op jit(solution)/shard_map/ppermute | solution.py:463
  180.9 25.9 %collective-permute-start.22 = (bf16[128,384]{1,0:T(8,128)(2,1)}, bf16[128,384]{1,0:T(8,128)(2,1)S(1)}, u32[]{:S(2)}, u32[]{:S(2)}) collective-permute-start(bf16[128,384]{1,0:T(8,128)(2,1)} %get-tuple-element.28), channel_id=1, source_target_pairs={{0,192},{4,196},{8,200},{12,204},{16,208},{20,212},{24,216},{28,22... | collective-permute-start | bytes 294920 | tf_op jit(solution)/shard_map/ppermute | solution.py:463
  209.5 15.1 %collective-permute-start.27 = (bf16[4,2,64,384]{3,2,1,0:T(8,128)(2,1)}, bf16[4,2,64,384]{3,2,1,0:T(8,128)(2,1)S(1)}, u32[]{:S(2)}, u32[]{:S(2)}) collective-permute-start(bf16[4,2,64,384]{3,2,1,0:T(8,128)(2,1)} %bitcast.41), channel_id=1, source_target_pairs={{0,8},{4,12},{8,16},{12,20},{16,24},{20,28},{24,0},{28,4},{32,40},... | collective-permute-start | bytes 1179656 | tf_op jit(solution)/shard_map/ppermute | solution.py:475
  211.6 27.3 %collective-permute-start.28 = (bf16[4,2,64,384]{3,2,1,0:T(8,128)(2,1)}, bf16[4,2,64,384]{3,2,1,0:T(8,128)(2,1)}, u32[]{:S(2)}, u32[]{:S(2)}) collective-permute-start(bf16[4,2,64,384]{3,2,1,0:T(8,128)(2,1)} %bitcast.42), channel_id=1, source_target_pairs={{0,16},{4,20},{8,24},{12,28},{16,0},{20,4},{24,8},{28,12},{32,48},... | collective-permute-start | bytes 1179656 | tf_op jit(solution)/shard_map/ppermute | solution.py:475
  214.2 36.1 %collective-permute-start.29 = (bf16[4,2,64,384]{3,2,1,0:T(8,128)(2,1)}, bf16[4,2,64,384]{3,2,1,0:T(8,128)(2,1)}, u32[]{:S(2)}, u32[]{:S(2)}) collective-permute-start(bf16[4,2,64,384]{3,2,1,0:T(8,128)(2,1)} %bitcast.43), channel_id=1, source_target_pairs={{0,24},{4,28},{8,0},{12,4},{16,8},{20,12},{24,16},{28,20},{32,56},... | collective-permute-start | bytes 1179656 | tf_op jit(solution)/shard_map/ppermute | solution.py:475
  257.1 22.6 %collective-permute-start.34 = (bf16[4,2,64,256]{3,2,1,0:T(8,128)(2,1)}, bf16[4,2,64,256]{3,2,1,0:T(8,128)(2,1)S(1)}, u32[]{:S(2)}, u32[]{:S(2)}) collective-permute-start(bf16[4,2,64,256]{3,2,1,0:T(8,128)(2,1)} %bitcast.46), channel_id=1, source_target_pairs={{0,16},{4,20},{8,24},{12,28},{16,0},{20,4},{24,8},{28,12},{32,48},... | collective-permute-start | bytes 786440 | tf_op jit(solution)/shard_map/ppermute | solution.py:475
  260.8 21.8 %collective-permute-start.35 = (bf16[4,2,64,256]{3,2,1,0:T(8,128)(2,1)}, bf16[4,2,64,256]{3,2,1,0:T(8,128)(2,1)S(1)}, u32[]{:S(2)}, u32[]{:S(2)}) collective-permute-start(bf16[4,2,64,256]{3,2,1,0:T(8,128)(2,1)} %bitcast.47), channel_id=1, source_target_pairs={{0,24},{4,28},{8,0},{12,4},{16,8},{20,12},{24,16},{28,20},{32,56},... | collective-permute-start | bytes 786440 | tf_op jit(solution)/shard_map/ppermute | solution.py:475
  262.4 20.2 %collective-permute-start.30 = (bf16[512,256]{1,0:T(8,128)(2,1)}, bf16[512,256]{1,0:T(8,128)(2,1)S(1)}, u32[]{:S(2)}, u32[]{:S(2)}) collective-permute-start(bf16[512,256]{1,0:T(8,128)(2,1)} %shared_hidden.1.h0), channel_id=1, source_target_pairs={{0,1},{1,0},{2,3},{3,2},{4,5},{5,4},{6,7},{7,6},{8,9},{9,8},{10,11... | collective-permute-start | bytes 786440 | tf_op jit(solution)/shard_map/ppermute | solution.py:493
  264.6 18.0 %collective-permute-start.32 = (bf16[512,256]{1,0:T(8,128)(2,1)S(1)}, bf16[512,256]{1,0:T(8,128)(2,1)S(1)}, u32[]{:S(2)}, u32[]{:S(2)}) collective-permute-start(bf16[512,256]{1,0:T(8,128)(2,1)S(1)} %collective-permute-done.31.h2), channel_id=1, source_target_pairs={{0,1},{1,0},{2,3},{3,2},{4,5},{5,4},{6,7},{7,6},{8,9},{9,8},{10,11... | collective-permute-start | bytes 786440 | tf_op jit(solution)/shard_map/ppermute | solution.py:494
  (54 other events, 533.6 us)
where the time goes:
time: 308 us; the launch traced here: 307 us
  waiting for transfers between devices  149 us (48%)
  starting transfers between devices  64.6 us (21%)
  blocking collectives  42.4 us (14%)
  Pallas kernels  41.8 us (14%)
  local copies, waits for them, and re-layouts  7.83 us (3%)
    ppermute x6, waiting for transfers between devices, body(): blocks.append(lax.ppermute(blocks[0], 'wide', moved(0, 0, 2 * k)))  50.9 us
    all_to_all x1, blocking collectives, body(): lax.all_to_all(outgoing, 'wide', 0, 0, tiled=True).reshape(SLOTS, COLS)  42.4 us
    ppermute x3, waiting for transfers between devices, body(): lax.ppermute(raw, 'wide', moved(0, i & 1, 0, i >> 1))  25.6 us
    ppermute x3, waiting for transfers between devices, body(): pieces[d] = lax.ppermute(pieces[d], 'wide', moved(d, 0, 0))  24.1 us
    ppermute x2, waiting for transfers between devices, body(): lax.ppermute(own[k * CHUNK_ROWS:(k + 1) * CHUNK_ROWS], 'narrow', Y_SWAP)  22 us
    ppermute x3, waiting for transfers between devices, body(): lax.ppermute(w, 'narrow', swap)  14.9 us
    ppermute x6, starting transfers between devices, body(): blocks.append(lax.ppermute(blocks[0], 'wide', moved(0, 0, 2 * k)))  14.9 us
    pallas_call x2, Pallas kernels, expert_hidden(): pl.pallas_call(hidden_kernel, grid_spec=pltpu.PrefetchScalarGridSpec(num_...  10.9 us
  transfers between devices with their start and end apart: 40, of which 18 were waited for; matrix products, arithmetic and copies ran while one was open for 0% of the time, Pallas kernels for 10%

commit v1 on v0

--- a/solution.py
+++ b/solution.py
@@ -172,21 +172,23 @@
 
 
 def stack_kernel(place_ref, *refs):
-    pieces, outs = refs[:8], refs[8:]
+    pieces, out_ref = refs[:8], refs[8]
     x = place_ref[1]
+    lanes = pieces[0].shape[1]
     for d in range(NX):
-        at = pl.ds((x - d) & 3, 1)
-        outs[0][at] = pieces[d][...][None]
-        outs[1][at] = pieces[NX + d][...][None]
+        at = (x - d) & 3
+        out_ref[pl.ds(at, 1), :, :lanes] = pieces[d][...][None]
+        out_ref[pl.ds(at, 1), :, lanes:] = pieces[NX + d][...][None]
 
 
 def stack(place, pieces):
     vmem = pl.BlockSpec(memory_space=pltpu.VMEM)
+    lanes = pieces[0].shape[1] + pieces[NX].shape[1]
     return pl.pallas_call(
         stack_kernel,
         in_specs=[pl.BlockSpec(memory_space=pltpu.SMEM)] + [vmem] * 8,
-        out_specs=[vmem] * 2,
-        out_shape=[jax.ShapeDtypeStruct((NX,) + pieces[i].shape, BF16) for i in (0, NX)],
+        out_specs=vmem,
+        out_shape=jax.ShapeDtypeStruct((NX, pieces[0].shape[0], lanes), BF16),
         name="stack",
     )(place, *pieces)
 
@@ -294,11 +296,11 @@
     )(pos, *hiddens, w_own, *w_others, *more)
 
 
-def fetch(blocks, w_ref, sems, z):
+def fetch(blocks, w_ref, sems, z, first):
     copies = []
     for step, block in enumerate(blocks):
-        to = w_ref.at[((z >> 1) - step) & (PAIRS - 1)]
-        copies.append(pltpu.make_async_copy(block, to, sems.at[step]))
+        part = block.at[:, :, :, pl.ds(first, w_ref.shape[4])]
+        copies.append(pltpu.make_async_copy(part, w_ref.at[((z >> 1) - step) & (PAIRS - 1)], sems.at[step]))
     for copy in copies:
         copy.start()
     for copy in copies:
@@ -308,7 +310,7 @@
 def shared_hidden_kernel(place_ref, t0, t1, t2, t3, *refs):
     blocks, (out_ref, w_ref, sems) = refs[:PAIRS], refs[PAIRS + 1 :]
     z = place_ref[3]
-    fetch(blocks, w_ref, sems, z)
+    fetch(blocks, w_ref, sems, z, 0)
     rows = PAIRS * w_ref.shape[3]
     lanes = w_ref.shape[4]
     fs = FS // (4 * NX)
@@ -323,8 +325,7 @@
     out_ref[...] = padded_to(hidden, out_ref.shape[1]).astype(BF16)
 
 
-def shared_hidden(place, toks, blocks, after, units):
-    lanes = blocks[0].shape[3]
+def shared_hidden(place, toks, blocks, after, lanes, units):
     vmem = pl.BlockSpec(memory_space=pltpu.VMEM)
     return pl.pallas_call(
         shared_hidden_kernel,
@@ -334,7 +335,7 @@
         out_specs=vmem,
         out_shape=jax.ShapeDtypeStruct((NX * TOK, units), BF16),
         scratch_shapes=[
-            pltpu.VMEM((PAIRS,) + blocks[0].shape, BF16),
+            pltpu.VMEM((PAIRS,) + blocks[0].shape[:3] + (lanes,), BF16),
             pltpu.SemaphoreType.DMA((PAIRS,)),
         ],
         cost_estimate=pl.CostEstimate(
@@ -348,7 +349,7 @@
     blocks, outs, (w_ref, sems) = refs[:PAIRS], refs[PAIRS + 1 : PAIRS + 5], refs[PAIRS + 5 :]
     n, z = place_ref[0], place_ref[3]
     units = w_ref.shape[4]
-    fetch(blocks, w_ref, sems, z)
+    fetch(blocks, w_ref, sems, z, blocks[0].shape[3] - units)
     rows = PAIRS * w_ref.shape[3]
     for half in range(NY):
         total = jnp.zeros((NX * TOK, rows), F32)
@@ -370,7 +371,7 @@
         out_specs=[vmem] * 4,
         out_shape=[jax.ShapeDtypeStruct((TOK, COLS), BF16)] * 4,
         scratch_shapes=[
-            pltpu.VMEM((PAIRS,) + blocks[0].shape, BF16),
+            pltpu.VMEM((PAIRS,) + blocks[0].shape[:3] + (units,), BF16),
             pltpu.SemaphoreType.DMA((PAIRS,)),
         ],
         cost_estimate=pl.CostEstimate(
@@ -466,13 +467,11 @@
         lax.ppermute(w, "narrow", swap)
         for w, swap in zip(cuts, (Y_SWAP, BOTH_SWAP, CORE_SWAP))
     ]
-    columns = stack(place, pieces)
-    inward, outward = [
-        [c.reshape(NX, NY, c.shape[1] // NY, c.shape[2])] for c in columns
-    ]
-    for blocks in (inward, outward):
-        for k in range(1, PAIRS):
-            blocks.append(lax.ppermute(blocks[0], "wide", moved(0, 0, 2 * k)))
+    column = stack(place, pieces)
+    column = column.reshape(NX, NY, column.shape[1] // NY, column.shape[2])
+    blocks = [column]
+    for k in range(1, PAIRS):
+        blocks.append(lax.ppermute(column, "wide", moved(0, 0, 2 * k)))
     toks = [tokens]
     for d in range(1, NX):
         toks.append(lax.ppermute(tokens, "wide", moved(d, 0, 0)))
@@ -488,7 +487,8 @@
         hidden_y = lax.ppermute(hidden, "narrow", Y_SWAP)
         hidden_core = lax.ppermute(hidden, "narrow", CORE_SWAP)
         hiddens.append([hidden, hidden_y, hidden_core])
-    common = shared_hidden(place, toks, inward, hiddens[-1][0], pieces[NX].shape[1])
+    lanes, units = pieces[0].shape[1], pieces[NX].shape[1]
+    common = shared_hidden(place, toks, blocks, hiddens[-1][0], lanes, units)
     common_y = lax.ppermute(common, "narrow", Y_SWAP)
     common_core = lax.ppermute(common, "narrow", CORE_SWAP)
     common_both = lax.ppermute(common_y, "narrow", CORE_SWAP)
@@ -499,7 +499,7 @@
         outputs = expert_columns(pos, k, hiddens[k], expert_down, others, outputs)
     returned = lax.all_to_all(outputs.reshape(EXPERTS, CAP, COLS), "wide", 0, 0, tiled=True)
 
-    shared = list(shared_columns(place, [common, common_core, common_y, common_both], outward, outputs))
+    shared = list(shared_columns(place, [common, common_core, common_y, common_both], blocks, outputs))
     for d in range(1, NX):
         shared[d] = lax.ppermute(shared[d], "wide", moved(-d, 0, 0))
     return combine(ids_t, gates_t, returned.reshape(SLOTS, COLS), shared)

time: 308 us -> 288 us (0.935)
  waiting for transfers between devices: 149 us -> 136 us
  starting transfers between devices: 64.6 us -> 58.2 us
    ppermute x3, waiting for transfers between devices: 24.1 us -> 0.01 us  [body(): pieces[d] = lax.ppermute(pieces[d], 'wide', moved(d, 0, 0))]
    ppermute x3, waiting for transfers between devices: 0.01 us -> 23.1 us  [body(): toks.append(lax.ppermute(tokens, 'wide', moved(d, 0, 0)))]
    ppermute x6 -> x3, waiting for transfers between devices: 50.9 us -> 28.9 us  [body(): blocks.append(lax.ppermute(column, 'wide', moved(0, 0, 2 * k)))]
    ppermute x6 -> x3, starting transfers between devices: 14.9 us -> 8.45 us  [body(): blocks.append(lax.ppermute(column, 'wide', moved(0, 0, 2 * k)))]
    ppermute x1, waiting for transfers between devices: 0.01 us -> 5.63 us  [body(): common_y = lax.ppermute(common, 'narrow', Y_SWAP)]
    ppermute x4, waiting for transfers between devices: 0.01 us -> 3.55 us  [body(): lax.ppermute(pieces[NX + d], ('wide', 'narrow'), turned_about(d))]
    unnamed x76 -> x72, local copies, waits for them, and re-layouts: 7.76 us -> 7.32 us
  transfers between devices with their start and end apart: 40 -> 37, of which waited for: 18 -> 17; matrix products, arithmetic and copies ran while one was open for 0% -> 0% of each run, Pallas kernels for 10% -> 11%
where the time goes in v1:
time: 288 us; the launch traced here: 287 us
  waiting for transfers between devices  136 us (47%)
  starting transfers between devices  58.2 us (20%)
  blocking collectives  42.4 us (15%)
  Pallas kernels  41.9 us (15%)
  local copies, waits for them, and re-layouts  7.39 us (3%)
    all_to_all x1, blocking collectives, body(): lax.all_to_all(outgoing, 'wide', 0, 0, tiled=True).reshape(SLOTS, COLS)  42.4 us
    ppermute x3, waiting for transfers between devices, body(): blocks.append(lax.ppermute(column, 'wide', moved(0, 0, 2 * k)))  28.9 us
    ppermute x3, waiting for transfers between devices, body(): lax.ppermute(raw, 'wide', moved(0, i & 1, 0, i >> 1))  25.6 us
    ppermute x3, waiting for transfers between devices, body(): toks.append(lax.ppermute(tokens, 'wide', moved(d, 0, 0)))  23.1 us
    ppermute x2, waiting for transfers between devices, body(): lax.ppermute(own[k * CHUNK_ROWS:(k + 1) * CHUNK_ROWS], 'narrow', Y_SWAP)  22 us
    ppermute x3, waiting for transfers between devices, body(): lax.ppermute(w, 'narrow', swap)  14.9 us
    pallas_call x2, Pallas kernels, expert_hidden(): pl.pallas_call(hidden_kernel, grid_spec=pltpu.PrefetchScalarGridSpec(num_...  10.9 us
    ppermute x4, starting transfers between devices, body(): lax.ppermute(pieces[NX + d], ('wide', 'narrow'), turned_about(d))  10.7 us
  transfers between devices with their start and end apart: 37, of which 17 were waited for; matrix products, arithmetic and copies ran while one was open for 0% of the time, Pallas kernels for 11%

profile of v1, /device:TPU:1, one launch (start us, length us, event | category | flops | bytes accessed | tf_op | source)
XLA Modules:
  0.0 287.2 jit_solution(9867748366255828325)
XLA Ops:
  2.8 42.4 %all_to_all.10 = bf16[64,16,512]{2,1,0:T(8,128)(2,1)S(1)} all-to-all(bf16[64,16,512]{2,1,0:T(8,128)(2,1)} %bitcast.42), channel_id=1, replica_groups=mesh['wide'=64,'narrow'=4] {'wide'}, dimensions={0} | all-to-all | bytes 2097152 | tf_op jit(solution)/shard_map/all_to_all | solution.py:458
  45.2 4.2 %collective-permute-start = (bf16[1024,512]{1,0:T(8,128)(2,1)S(1)}, bf16[1024,512]{1,0:T(8,128)(2,1)S(1)}, u32[]{:S(2)}, u32[]{:S(2)}) collective-permute-start(bf16[1024,512]{1,0:T(8,128)(2,1)S(1)} %bitcast.32), channel_id=1, source_target_pairs={{0,1},{1,0},{2,3},{3,2},{4,5},{5,4},{6,7},{7,6},{8,9},{9,8},{10,11... | collective-permute-start | bytes 3145736 | tf_op jit(solution)/shard_map/ppermute | solution.py:482
  51.0 12.0 %collective-permute-done.9.x2 = bf16[512,512]{1,0:T(8,128)(2,1)S(1)} collective-permute-done((bf16[512,512]{1,0:T(8,128)(2,1)S(1)}, bf16[512,512]{1,0:T(8,128)(2,1)S(1)}, u32[]{:S(2)}, u32[]{:S(2)}) %collective-permute-start.9) | collective-permute-done | bytes 524320 | tf_op jit(solution)/shard_map/ppermute | solution.py:481
  64.4 10.0 %collective-permute-done.1.x2 = bf16[512,512]{1,0:T(8,128)(2,1)} collective-permute-done((bf16[512,512]{1,0:T(8,128)(2,1)S(1)}, bf16[512,512]{1,0:T(8,128)(2,1)}, u32[]{:S(2)}, u32[]{:S(2)}) %collective-permute-start.1) | collective-permute-done | bytes 524320 | tf_op jit(solution)/shard_map/ppermute | solution.py:481
  78.9 5.4 %hidden.3.h0 = bf16[512,384]{1,0:T(8,128)(2,1)} custom-call(s32[1]{0:T(128)} %bitcast.2.pos_ref, bf16[1024,512]{1,0:T(8,128)(2,1)} %bitcast.33, bf16[1024,512]{1,0:T(8,128)(2,1)} %copy-done.1, bf16[512,512]{1,0:T(8,128)(2,1)} %copy-done.11, bf16[512,512]{1,0:T(8,128)(2,1)} %collective-permute-done.10.x3, bf16[1,352,2048]{2,1,0:T(8,128)(2,1)} %bitcast.16, ...), custom_call_target="tpu_custom_call" | custom-call | flops 1476395008 | bytes 6000000 | tf_op jit(solution)/shard_map/hidden/pallas_call | solution.py:247
  85.5 5.5 %hidden.2.h0.refs_4_ = bf16[512,384]{1,0:T(8,128)(2,1)} custom-call(s32[1]{0:T(128)} %bitcast.2.pos_ref, bf16[1024,512]{1,0:T(8,128)(2,1)} %bitcast.34, bf16[1024,512]{1,0:T(8,128)(2,1)} %copy-done.1, bf16[512,512]{1,0:T(8,128)(2,1)} %collective-permute-done.1.x2, bf16[512,512]{1,0:T(8,128)(2,1)} %collective-permute-done.2.x3, ...), custom_call_target="tpu_custom_call" | custom-call | flops 1476395008 | bytes 6000000 | tf_op jit(solution)/shard_map/hidden/pallas_call | solution.py:247
  97.6 14.9 %collective-permute-done.7.w2 = bf16[352,512]{1,0:T(8,128)(2,1)S(1)} collective-permute-done((bf16[352,512]{1,0:T(8,128)(2,1)S(1)}, bf16[352,512]{1,0:T(8,128)(2,1)S(1)}, u32[]{:S(2)}, u32[]{:S(2)}) %collective-permute-start.7) | collective-permute-done | bytes 360480 | tf_op jit(solution)/shard_map/ppermute | solution.py:467
  113.9 3.9 %down.2.rest_0_ = bf16[1024,512]{1,0:T(8,128)(2,1)} custom-call(s32[1]{0:T(128)} %bitcast.2.pos_ref, bf16[512,384]{1,0:T(8,128)(2,1)} %hidden.3.h0, bf16[512,384]{1,0:T(8,128)(2,1)} %copy-done.17, bf16[512,384]{1,0:T(8,128)(2,1)} %collective-permute-done.12.h2, bf16[512,384]{1,0:T(8,128)(2,1)} %copy-done.18, bf16[1,352,2048]{2,1,0:T(8,128)(2,1)} %w0.3, ...), custom_call_target="tpu_custom_call" | custom-call | flops 738197504 | bytes 4000000 | tf_op jit(solution)/shard_map/down/pallas_call | solution.py:279
  119.3 3.9 %down.3.refs_4_ = bf16[1024,512]{1,0:T(8,128)(2,1)} custom-call(s32[1]{0:T(128)} %bitcast.2.pos_ref, bf16[512,384]{1,0:T(8,128)(2,1)} %hidden.2.h0.refs_4_, bf16[512,384]{1,0:T(8,128)(2,1)} %copy-done.14, bf16[512,384]{1,0:T(8,128)(2,1)} %copy-done.16, bf16[512,384]{1,0:T(8,128)(2,1)} %copy-done.15, ...), custom_call_target="tpu_custom_call", output_to_operand_aliasing={{}: (9, {})} | custom-call | flops 738197504 | bytes 4000000 | tf_op jit(solution)/shard_map/down/pallas_call | solution.py:279
  123.2 6.1 %all-to-all-start.1 = ((bf16[64,16,512]{2,1,0:T(8,128)(2,1)}), bf16[64,16,512]{2,1,0:T(8,128)(2,1)S(1)}, u32[]{:S(2)}, u32[]{:S(2)}) async-start(bf16[64,16,512]{2,1,0:T(8,128)(2,1)} %bitcast.35), calls=%async_computation.1 | async-start | bytes 2097152 | tf_op jit(solution)/shard_map/all_to_all | solution.py:500
  136.8 5.2 %collective-permute-done.17.refs_1_ = bf16[4,32,640]{2,1,0:T(8,128)(2,1)S(1)} collective-permute-done((bf16[4,32,640]{2,1,0:T(8,128)(2,1)}, bf16[4,32,640]{2,1,0:T(8,128)(2,1)S(1)}, u32[]{:S(2)}, u32[]{:S(2)}) %collective-permute-start.17) | collective-permute-done | bytes 163872 | tf_op jit(solution)/shard_map/ppermute | solution.py:455
  141.9 14.5 %collective-permute-done.18.refs_2_ = bf16[4,32,640]{2,1,0:T(8,128)(2,1)S(1)} collective-permute-done((bf16[4,32,640]{2,1,0:T(8,128)(2,1)}, bf16[4,32,640]{2,1,0:T(8,128)(2,1)S(1)}, u32[]{:S(2)}, u32[]{:S(2)}) %collective-permute-start.18) | collective-permute-done | bytes 163872 | tf_op jit(solution)/shard_map/ppermute | solution.py:455
  156.5 5.9 %collective-permute-done.19.refs_3_ = bf16[4,32,640]{2,1,0:T(8,128)(2,1)S(1)} collective-permute-done((bf16[4,32,640]{2,1,0:T(8,128)(2,1)}, bf16[4,32,640]{2,1,0:T(8,128)(2,1)S(1)}, u32[]{:S(2)}, u32[]{:S(2)}) %collective-permute-start.19) | collective-permute-done | bytes 163872 | tf_op jit(solution)/shard_map/ppermute | solution.py:455
  165.1 4.3 %collective-permute-start.23 = (bf16[128,256]{1,0:T(8,128)(2,1)}, bf16[128,256]{1,0:T(8,128)(2,1)S(1)}, u32[]{:S(2)}, u32[]{:S(2)}) collective-permute-start(bf16[128,256]{1,0:T(8,128)(2,1)} %get-tuple-element.27), channel_id=1, source_target_pairs={{0,0},{1,64},{2,128},{3,192},{4,4},{5,68},{6,132},{7,196},{8,8},{9... | collective-permute-start | bytes 196616 | tf_op jit(solution)/shard_map/ppermute | solution.py:462
  179.1 3.5 %collective-permute-done.26.refs_7_ = bf16[128,256]{1,0:T(8,128)(2,1)S(1)} collective-permute-done((bf16[128,256]{1,0:T(8,128)(2,1)}, bf16[128,256]{1,0:T(8,128)(2,1)S(1)}, u32[]{:S(2)}, u32[]{:S(2)}) %collective-permute-start.26) | collective-permute-done | bytes 65568 | tf_op jit(solution)/shard_map/ppermute | solution.py:462
  187.5 3.5 %collective-permute-start.28 = (bf16[4,2,64,640]{3,2,1,0:T(8,128)(2,1)}, bf16[4,2,64,640]{3,2,1,0:T(8,128)(2,1)S(1)}, u32[]{:S(2)}, u32[]{:S(2)}) collective-permute-start(bf16[4,2,64,640]{3,2,1,0:T(8,128)(2,1)} %bitcast.37), channel_id=1, source_target_pairs={{0,16},{4,20},{8,24},{12,28},{16,0},{20,4},{24,8},{28,12},{32,48},... | collective-permute-start | bytes 1966088 | tf_op jit(solution)/shard_map/ppermute | solution.py:474
  197.2 9.9 %collective-permute-done.15.t2 = bf16[128,2048]{1,0:T(8,128)(2,1)S(1)} collective-permute-done((bf16[128,2048]{1,0:T(8,128)(2,1)S(1)}, bf16[128,2048]{1,0:T(8,128)(2,1)S(1)}, u32[]{:S(2)}, u32[]{:S(2)}) %collective-permute-start.15) | collective-permute-done | bytes 524320 | tf_op jit(solution)/shard_map/ppermute | solution.py:477
  207.1 13.2 %collective-permute-done.16.t3 = bf16[128,2048]{1,0:T(8,128)(2,1)S(1)} collective-permute-done((bf16[128,2048]{1,0:T(8,128)(2,1)S(1)}, bf16[128,2048]{1,0:T(8,128)(2,1)S(1)}, u32[]{:S(2)}, u32[]{:S(2)}) %collective-permute-start.16) | collective-permute-done | bytes 524320 | tf_op jit(solution)/shard_map/ppermute | solution.py:477
  220.3 17.9 %collective-permute-done.28.refs_2_ = bf16[4,2,64,640]{3,2,1,0:T(8,128)(2,1)S(1)} collective-permute-done((bf16[4,2,64,640]{3,2,1,0:T(8,128)(2,1)}, bf16[4,2,64,640]{3,2,1,0:T(8,128)(2,1)S(1)}, u32[]{:S(2)}, u32[]{:S(2)}) %collective-permute-start.28) | collective-permute-done | bytes 655392 | tf_op jit(solution)/shard_map/ppermute | solution.py:474
  238.3 11.0 %collective-permute-done.29.refs_3_ = bf16[4,2,64,640]{3,2,1,0:T(8,128)(2,1)S(1)} collective-permute-done((bf16[4,2,64,640]{3,2,1,0:T(8,128)(2,1)}, bf16[4,2,64,640]{3,2,1,0:T(8,128)(2,1)S(1)}, u32[]{:S(2)}, u32[]{:S(2)}) %collective-permute-start.29) | collective-permute-done | bytes 655392 | tf_op jit(solution)/shard_map/ppermute | solution.py:474
  250.1 4.9 %shared_hidden.1.h0 = bf16[512,256]{1,0:T(8,128)(2,1)} custom-call(s32[4]{0:T(128)} %pad_add_fusion.place_ref, bf16[128,2048]{1,0:T(8,128)(2,1)} %t0.1, bf16[128,2048]{1,0:T(8,128)(2,1)} %collective-permute-done.14.t1, bf16[128,2048]{1,0:T(8,128)(2,1)} %copy-done.12, bf16[128,2048]{1,0:T(8,128)(2,1)} %copy-done.13, bf16[4,2,64,640]{3,2,1,0:T(8,128)(2,1)} %bitcast.39, ...), custom_call_target="tpu_custom_call" | custom-call | flops 805306368 | bytes 5000000 | tf_op jit(solution)/shard_map/shared_hidden/pallas_call | solution.py:330
  258.4 5.6 %collective-permute-done.31.h2 = bf16[512,256]{1,0:T(8,128)(2,1)S(1)} collective-permute-done((bf16[512,256]{1,0:T(8,128)(2,1)}, bf16[512,256]{1,0:T(8,128)(2,1)S(1)}, u32[]{:S(2)}, u32[]{:S(2)}) %collective-permute-start.31) | collective-permute-done | bytes 262176 | tf_op jit(solution)/shard_map/ppermute | solution.py:492
  267.0 3.8 %shared_down.1 = (bf16[128,512]{1,0:T(8,128)(2,1)}, bf16[128,512]{1,0:T(8,128)(2,1)}, bf16[128,512]{1,0:T(8,128)(2,1)}, bf16[128,512]{1,0:T(8,128)(2,1)}) custom-call(s32[4]{0:T(128)} %pad_add_fusion.place_ref, bf16[512,256]{1,0:T(8,128)(2,1)} %shared_hidden.1.h0, bf16[512,256]{1,0:T(8,128)(2,1)} %copy-done.20, bf16[512,256]{1,0:T(8,128)(2,1)} %copy-done.19, ...), custom_call_target="tpu_custom_call" | custom-call | flops 536870912 | bytes 4000000 | tf_op jit(solution)/shard_map/shared_down/pallas_call | solution.py:366
  283.6 3.6 %combine.1 = bf16[128,512]{1,0:T(8,128)(2,1)} custom-call(s32[6,128]{1,0:T(8,128)} %bitcast.47, f32[6,128]{1,0:T(8,128)} %bitcast.48, bf16[1024,512]{1,0:T(8,128)(2,1)} %bitcast.41, bf16[128,512]{1,0:T(8,128)(2,1)} %get-tuple-element.31.s0, bf16[128,512]{1,0:T(8,128)(2,1)} %copy-done.25, bf16[128,512]{1,0:T(8,128)(2,1)} %copy-done.26, ...), custom_call_target="tpu_custom_call" | custom-call | tf_op jit(solution)/shard_map/combine/pallas_call | solution.py:427
  (137 shorter events, 71.8 us)
Async XLA Ops:
  45.2 32.7 %collective-permute-start = (bf16[1024,512]{1,0:T(8,128)(2,1)S(1)}, bf16[1024,512]{1,0:T(8,128)(2,1)S(1)}, u32[]{:S(2)}, u32[]{:S(2)}) collective-permute-start(bf16[1024,512]{1,0:T(8,128)(2,1)S(1)} %bitcast.32), channel_id=1, source_target_pairs={{0,1},{1,0},{2,3},{3,2},{4,5},{5,4},{6,7},{7,6},{8,9},{9,8},{10,11... | collective-permute-start | bytes 3145736 | tf_op jit(solution)/shard_map/ppermute | solution.py:482
  49.5 13.6 %collective-permute-start.9 = (bf16[512,512]{1,0:T(8,128)(2,1)S(1)}, bf16[512,512]{1,0:T(8,128)(2,1)S(1)}, u32[]{:S(2)}, u32[]{:S(2)}) collective-permute-start(bf16[512,512]{1,0:T(8,128)(2,1)S(1)} %bitcast.44), channel_id=1, source_target_pairs={{0,2},{2,0},{1,3},{3,1},{4,6},{6,4},{5,7},{7,5},{8,10},{10,8},{9,1... | collective-permute-start | bytes 1572872 | tf_op jit(solution)/shard_map/ppermute | solution.py:481
  50.0 24.4 %collective-permute-start.1 = (bf16[512,512]{1,0:T(8,128)(2,1)S(1)}, bf16[512,512]{1,0:T(8,128)(2,1)}, u32[]{:S(2)}, u32[]{:S(2)}) collective-permute-start(bf16[512,512]{1,0:T(8,128)(2,1)S(1)} %bitcast.43), channel_id=1, source_target_pairs={{0,2},{2,0},{1,3},{3,1},{4,6},{6,4},{5,7},{7,5},{8,10},{10,8},{9,1... | collective-permute-start | bytes 1572872 | tf_op jit(solution)/shard_map/ppermute | solution.py:481
  63.0 14.9 %collective-permute-start.10 = (bf16[512,512]{1,0:T(8,128)(2,1)S(1)}, bf16[512,512]{1,0:T(8,128)(2,1)}, u32[]{:S(2)}, u32[]{:S(2)}) collective-permute-start(bf16[512,512]{1,0:T(8,128)(2,1)S(1)} %collective-permute-done.9.x2), channel_id=1, source_target_pairs={{0,1},{1,0},{2,3},{3,2},{4,5},{5,4},{6,7},{7,6},{8,9},{9,8},{10,11... | collective-permute-start | bytes 1572872 | tf_op jit(solution)/shard_map/ppermute | solution.py:485
  74.4 11.2 %collective-permute-start.2 = (bf16[512,512]{1,0:T(8,128)(2,1)}, bf16[512,512]{1,0:T(8,128)(2,1)}, u32[]{:S(2)}, u32[]{:S(2)}) collective-permute-start(bf16[512,512]{1,0:T(8,128)(2,1)} %collective-permute-done.1.x2), channel_id=1, source_target_pairs={{0,1},{1,0},{2,3},{3,2},{4,5},{5,4},{6,7},{7,6},{8,9},{9,8},{10,11... | collective-permute-start | bytes 1572872 | tf_op jit(solution)/shard_map/ppermute | solution.py:485
  77.5 19.9 %collective-permute-start.6 = (bf16[352,512]{1,0:T(8,128)(2,1)}, bf16[352,512]{1,0:T(8,128)(2,1)S(1)}, u32[]{:S(2)}, u32[]{:S(2)}) collective-permute-start(bf16[352,512]{1,0:T(8,128)(2,1)} %get-tuple-element.20), channel_id=1, source_target_pairs={{0,2},{2,0},{1,3},{3,1},{4,6},{6,4},{5,7},{7,5},{8,10},{10,8},{9,1... | collective-permute-start | bytes 1081352 | tf_op jit(solution)/shard_map/ppermute | solution.py:467
  84.4 11.7 %collective-permute-start.11 = (bf16[512,384]{1,0:T(8,128)(2,1)}, bf16[512,384]{1,0:T(8,128)(2,1)S(1)}, u32[]{:S(2)}, u32[]{:S(2)}) collective-permute-start(bf16[512,384]{1,0:T(8,128)(2,1)} %hidden.3.h0), channel_id=1, source_target_pairs={{0,2},{2,0},{1,3},{3,1},{4,6},{6,4},{5,7},{7,5},{8,10},{10,8},{9,1... | collective-permute-start | bytes 1179656 | tf_op jit(solution)/shard_map/ppermute | solution.py:487
  91.0 21.7 %collective-permute-start.3 = (bf16[512,384]{1,0:T(8,128)(2,1)}, bf16[512,384]{1,0:T(8,128)(2,1)S(1)}, u32[]{:S(2)}, u32[]{:S(2)}) collective-permute-start(bf16[512,384]{1,0:T(8,128)(2,1)} %hidden.2.h0.refs_4_), channel_id=1, source_target_pairs={{0,2},{2,0},{1,3},{3,1},{4,6},{6,4},{5,7},{7,5},{8,10},{10,8},{9,1... | collective-permute-start | bytes 1179656 | tf_op jit(solution)/shard_map/ppermute | solution.py:487
  91.4 21.0 %collective-permute-start.7 = (bf16[352,512]{1,0:T(8,128)(2,1)S(1)}, bf16[352,512]{1,0:T(8,128)(2,1)S(1)}, u32[]{:S(2)}, u32[]{:S(2)}) collective-permute-start(bf16[352,512]{1,0:T(8,128)(2,1)S(1)} %copy-done.35), channel_id=1, source_target_pairs={{0,3},{3,0},{1,2},{2,1},{4,7},{7,4},{5,6},{6,5},{8,11},{11,8},{9,1... | collective-permute-start | bytes 1081352 | tf_op jit(solution)/shard_map/ppermute | solution.py:467
  93.2 19.7 %collective-permute-start.13 = (bf16[512,384]{1,0:T(8,128)(2,1)S(1)}, bf16[512,384]{1,0:T(8,128)(2,1)S(1)}, u32[]{:S(2)}, u32[]{:S(2)}) collective-permute-start(bf16[512,384]{1,0:T(8,128)(2,1)S(1)} %copy-done.7), channel_id=1, source_target_pairs={{0,1},{1,0},{2,3},{3,2},{4,5},{5,4},{6,7},{7,6},{8,9},{9,8},{10,11... | collective-permute-start | bytes 1179656 | tf_op jit(solution)/shard_map/ppermute | solution.py:488
  96.1 17.6 %collective-permute-start.12 = (bf16[512,384]{1,0:T(8,128)(2,1)S(1)}, bf16[512,384]{1,0:T(8,128)(2,1)}, u32[]{:S(2)}, u32[]{:S(2)}) collective-permute-start(bf16[512,384]{1,0:T(8,128)(2,1)S(1)} %collective-permute-done.11.h1), channel_id=1, source_target_pairs={{0,1},{1,0},{2,3},{3,2},{4,5},{5,4},{6,7},{7,6},{8,9},{9,8},{10,11... | collective-permute-start | bytes 1179656 | tf_op jit(solution)/shard_map/ppermute | solution.py:497
  97.5 15.5 %collective-permute-start.8 = (bf16[352,512]{1,0:T(8,128)(2,1)}, bf16[352,512]{1,0:T(8,128)(2,1)S(1)}, u32[]{:S(2)}, u32[]{:S(2)}) collective-permute-start(bf16[352,512]{1,0:T(8,128)(2,1)} %get-tuple-element.22), channel_id=1, source_target_pairs={{0,1},{1,0},{2,3},{3,2},{4,5},{5,4},{6,7},{7,6},{8,9},{9,8},{10,11... | collective-permute-start | bytes 1081352 | tf_op jit(solution)/shard_map/ppermute | solution.py:467
  123.2 159.4 %all-to-all-start.1 = ((bf16[64,16,512]{2,1,0:T(8,128)(2,1)}), bf16[64,16,512]{2,1,0:T(8,128)(2,1)S(1)}, u32[]{:S(2)}, u32[]{:S(2)}) async-start(bf16[64,16,512]{2,1,0:T(8,128)(2,1)} %bitcast.35), calls=%async_computation.1 | async-start | bytes 2097152 | tf_op jit(solution)/shard_map/all_to_all | solution.py:500
  129.3 65.1 %collective-permute-start.14 = (bf16[128,2048]{1,0:T(8,128)(2,1)S(1)}, bf16[128,2048]{1,0:T(8,128)(2,1)}, u32[]{:S(2)}, u32[]{:S(2)}) collective-permute-start(bf16[128,2048]{1,0:T(8,128)(2,1)S(1)} %copy-done.6), channel_id=1, source_target_pairs={{0,64},{4,68},{8,72},{12,76},{16,80},{20,84},{24,88},{28,92},{32,9... | collective-permute-start | bytes 1572872 | tf_op jit(solution)/shard_map/ppermute | solution.py:477
  132.0 10.0 %collective-permute-start.17 = (bf16[4,32,640]{2,1,0:T(8,128)(2,1)}, bf16[4,32,640]{2,1,0:T(8,128)(2,1)S(1)}, u32[]{:S(2)}, u32[]{:S(2)}) collective-permute-start(bf16[4,32,640]{2,1,0:T(8,128)(2,1)} %pack.1.refs_0_), channel_id=1, source_target_pairs={{0,32},{4,36},{8,40},{12,44},{16,48},{20,52},{24,56},{28,60},{32,0... | collective-permute-start | bytes 491528 | tf_op jit(solution)/shard_map/ppermute | solution.py:455
  134.7 21.8 %collective-permute-start.18 = (bf16[4,32,640]{2,1,0:T(8,128)(2,1)}, bf16[4,32,640]{2,1,0:T(8,128)(2,1)S(1)}, u32[]{:S(2)}, u32[]{:S(2)}) collective-permute-start(bf16[4,32,640]{2,1,0:T(8,128)(2,1)} %pack.1.refs_0_), channel_id=1, source_target_pairs={{0,4},{4,0},{8,12},{12,8},{16,20},{20,16},{24,28},{28,24},{32,36},... | collective-permute-start | bytes 491528 | tf_op jit(solution)/shard_map/ppermute | solution.py:455
  135.9 26.5 %collective-permute-start.19 = (bf16[4,32,640]{2,1,0:T(8,128)(2,1)}, bf16[4,32,640]{2,1,0:T(8,128)(2,1)S(1)}, u32[]{:S(2)}, u32[]{:S(2)}) collective-permute-start(bf16[4,32,640]{2,1,0:T(8,128)(2,1)} %pack.1.refs_0_), channel_id=1, source_target_pairs={{0,36},{4,32},{8,44},{12,40},{16,52},{20,48},{24,60},{28,56},{32,4... | collective-permute-start | bytes 491528 | tf_op jit(solution)/shard_map/ppermute | solution.py:455
  185.4 34.9 %collective-permute-start.27 = (bf16[4,2,64,640]{3,2,1,0:T(8,128)(2,1)}, bf16[4,2,64,640]{3,2,1,0:T(8,128)(2,1)S(1)}, u32[]{:S(2)}, u32[]{:S(2)}) collective-permute-start(bf16[4,2,64,640]{3,2,1,0:T(8,128)(2,1)} %bitcast.36), channel_id=1, source_target_pairs={{0,8},{4,12},{8,16},{12,20},{16,24},{20,28},{24,0},{28,4},{32,40},... | collective-permute-start | bytes 1966088 | tf_op jit(solution)/shard_map/ppermute | solution.py:474
  187.5 50.8 %collective-permute-start.28 = (bf16[4,2,64,640]{3,2,1,0:T(8,128)(2,1)}, bf16[4,2,64,640]{3,2,1,0:T(8,128)(2,1)S(1)}, u32[]{:S(2)}, u32[]{:S(2)}) collective-permute-start(bf16[4,2,64,640]{3,2,1,0:T(8,128)(2,1)} %bitcast.37), channel_id=1, source_target_pairs={{0,16},{4,20},{8,24},{12,28},{16,0},{20,4},{24,8},{28,12},{32,48},... | collective-permute-start | bytes 1966088 | tf_op jit(solution)/shard_map/ppermute | solution.py:474
  190.9 58.3 %collective-permute-start.29 = (bf16[4,2,64,640]{3,2,1,0:T(8,128)(2,1)}, bf16[4,2,64,640]{3,2,1,0:T(8,128)(2,1)S(1)}, u32[]{:S(2)}, u32[]{:S(2)}) collective-permute-start(bf16[4,2,64,640]{3,2,1,0:T(8,128)(2,1)} %bitcast.38), channel_id=1, source_target_pairs={{0,24},{4,28},{8,0},{12,4},{16,8},{20,12},{24,16},{28,20},{32,56},... | collective-permute-start | bytes 1966088 | tf_op jit(solution)/shard_map/ppermute | solution.py:474
  193.8 13.3 %collective-permute-start.15 = (bf16[128,2048]{1,0:T(8,128)(2,1)S(1)}, bf16[128,2048]{1,0:T(8,128)(2,1)S(1)}, u32[]{:S(2)}, u32[]{:S(2)}) collective-permute-start(bf16[128,2048]{1,0:T(8,128)(2,1)S(1)} %copy-done.6), channel_id=1, source_target_pairs={{0,128},{4,132},{8,136},{12,140},{16,144},{20,148},{24,152},{28,15... | collective-permute-start | bytes 1572872 | tf_op jit(solution)/shard_map/ppermute | solution.py:477
  194.4 25.9 %collective-permute-start.16 = (bf16[128,2048]{1,0:T(8,128)(2,1)S(1)}, bf16[128,2048]{1,0:T(8,128)(2,1)S(1)}, u32[]{:S(2)}, u32[]{:S(2)}) collective-permute-start(bf16[128,2048]{1,0:T(8,128)(2,1)S(1)} %copy-done.6), channel_id=1, source_target_pairs={{0,192},{4,196},{8,200},{12,204},{16,208},{20,212},{24,216},{28,22... | collective-permute-start | bytes 1572872 | tf_op jit(solution)/shard_map/ppermute | solution.py:477
  255.0 9.0 %collective-permute-start.31 = (bf16[512,256]{1,0:T(8,128)(2,1)}, bf16[512,256]{1,0:T(8,128)(2,1)S(1)}, u32[]{:S(2)}, u32[]{:S(2)}) collective-permute-start(bf16[512,256]{1,0:T(8,128)(2,1)} %shared_hidden.1.h0), channel_id=1, source_target_pairs={{0,2},{2,0},{1,3},{3,1},{4,6},{6,4},{5,7},{7,5},{8,10},{10,8},{9,1... | collective-permute-start | bytes 786440 | tf_op jit(solution)/shard_map/ppermute | solution.py:492
  273.2 9.4 %collective-permute-start.35 = (bf16[128,512]{1,0:T(8,128)(2,1)}, bf16[128,512]{1,0:T(8,128)(2,1)S(1)}, u32[]{:S(2)}, u32[]{:S(2)}) collective-permute-start(bf16[128,512]{1,0:T(8,128)(2,1)} %get-tuple-element.34), channel_id=1, source_target_pairs={{0,64},{4,68},{8,72},{12,76},{16,80},{20,84},{24,88},{28,92},{32,9... | collective-permute-start | bytes 393224 | tf_op jit(solution)/shard_map/ppermute | solution.py:504
  (49 other events, 351.4 us)

commit v2 on v1

--- a/solution.py
+++ b/solution.py
@@ -395,7 +395,7 @@
     return total
 
 
-def combine_kernel(ids_ref, gw_ref, ret_ref, s0, s1, s2, s3, out_ref):
+def weigh_kernel(ids_ref, gw_ref, out_ref):
     ids = turned(ids_ref[...].astype(F32))
     gates = turned(gw_ref[...])
     named = named_counts(ids, (TOK, EXPERTS), 1)
@@ -410,25 +410,37 @@
     spread = jnp.where((r >> 4) == e, 1.0, 0.0).astype(BF16)
     slot = (lax.broadcasted_iota(jnp.int32, (TOK, SLOTS), 1) & 15).astype(F32)
     hit = dot(keys, spread) == slot
+    rest = weight
+    for i in range(3):
+        part = rest.astype(BF16)
+        rest = rest - part.astype(F32)
+        out_ref[i] = jnp.where(hit, dot(part, spread), 0.0).astype(BF16)
+
+
+def weigh(ids, gate_weights):
+    return pl.pallas_call(
+        weigh_kernel,
+        out_shape=jax.ShapeDtypeStruct((3, TOK, SLOTS), BF16),
+        name="weigh",
+    )(ids, gate_weights)
+
+
+def combine_kernel(rows_ref, ret_ref, s0, s1, s2, s3, out_ref):
     ret = ret_ref[...]
     total = s0[...].astype(F32)
     for part in (s1, s2, s3):
         total = total + part[...].astype(F32)
-    rest = weight
-    for _ in range(3):
-        part = rest.astype(BF16)
-        rest = rest - part.astype(F32)
-        row = jnp.where(hit, dot(part, spread), 0.0).astype(BF16)
-        total = total + dot(row, ret)
+    for i in range(3):
+        total = total + dot(rows_ref[i], ret)
     out_ref[...] = total.astype(BF16)
 
 
-def combine(ids, gate_weights, returned, shared):
+def combine(rows, returned, shared):
     return pl.pallas_call(
         combine_kernel,
         out_shape=jax.ShapeDtypeStruct((TOK, COLS), BF16),
         name="combine",
-    )(ids, gate_weights, returned, *shared)
+    )(rows, returned, *shared)
 
 
 def body(
@@ -502,7 +514,8 @@
     shared = list(shared_columns(place, [common, common_core, common_y, common_both], blocks, outputs))
     for d in range(1, NX):
         shared[d] = lax.ppermute(shared[d], "wide", moved(-d, 0, 0))
-    return combine(ids_t, gates_t, returned.reshape(SLOTS, COLS), shared)
+    rows = weigh(ids_t, gates_t)
+    return combine(rows, returned.reshape(SLOTS, COLS), shared)
 
 
 def solution(mesh):

time: 288 us -> 287 us (level)
  transfers between devices with their start and end apart: 37 -> 37, of which waited for: 17 -> 17; matrix products, arithmetic and copies ran while one was open for 0% -> 0% of each run, Pallas kernels for 11% -> 12%
where the time goes in v2:
time: 287 us; the launch traced here: 286 us
  waiting for transfers between devices  134 us (47%)
  starting transfers between devices  58.2 us (20%)
  Pallas kernels  43.6 us (15%)
  blocking collectives  42.4 us (15%)
  local copies, waits for them, and re-layouts  7.39 us (3%)
    all_to_all x1, blocking collectives, body(): lax.all_to_all(outgoing, 'wide', 0, 0, tiled=True).reshape(SLOTS, COLS)  42.4 us
    ppermute x3, waiting for transfers between devices, body(): blocks.append(lax.ppermute(column, 'wide', moved(0, 0, 2 * k)))  28.9 us
    ppermute x3, waiting for transfers between devices, body(): lax.ppermute(raw, 'wide', moved(0, i & 1, 0, i >> 1))  25.6 us
    ppermute x3, waiting for transfers between devices, body(): toks.append(lax.ppermute(tokens, 'wide', moved(d, 0, 0)))  23.1 us
    ppermute x2, waiting for transfers between devices, body(): lax.ppermute(own[k * CHUNK_ROWS:(k + 1) * CHUNK_ROWS], 'narrow', Y_SWAP)  22 us
    ppermute x3, waiting for transfers between devices, body(): lax.ppermute(w, 'narrow', swap)  14.9 us
    pallas_call x2, Pallas kernels, expert_hidden(): pl.pallas_call(hidden_kernel, grid_spec=pltpu.PrefetchScalarGridSpec(num_...  10.9 us
    ppermute x4, starting transfers between devices, body(): lax.ppermute(pieces[NX + d], ('wide', 'narrow'), turned_about(d))  10.7 us
  transfers between devices with their start and end apart: 37, of which 17 were waited for; matrix products, arithmetic and copies ran while one was open for 0% of the time, Pallas kernels for 12%

profile of v2, /device:TPU:1, one launch (start us, length us, event | category | flops | bytes accessed | tf_op | source)
XLA Modules:
  0.0 286.4 jit_solution(2689217772421845621)
XLA Ops:
  2.8 42.4 %all_to_all.10 = bf16[64,16,512]{2,1,0:T(8,128)(2,1)S(1)} all-to-all(bf16[64,16,512]{2,1,0:T(8,128)(2,1)} %bitcast.42), channel_id=1, replica_groups=mesh['wide'=64,'narrow'=4] {'wide'}, dimensions={0} | all-to-all | bytes 2097152 | tf_op jit(solution)/shard_map/all_to_all | solution.py:470
  45.2 4.2 %collective-permute-start = (bf16[1024,512]{1,0:T(8,128)(2,1)S(1)}, bf16[1024,512]{1,0:T(8,128)(2,1)S(1)}, u32[]{:S(2)}, u32[]{:S(2)}) collective-permute-start(bf16[1024,512]{1,0:T(8,128)(2,1)S(1)} %bitcast.32), channel_id=1, source_target_pairs={{0,1},{1,0},{2,3},{3,2},{4,5},{5,4},{6,7},{7,6},{8,9},{9,8},{10,11... | collective-permute-start | bytes 3145736 | tf_op jit(solution)/shard_map/ppermute | solution.py:494
  51.0 12.0 %collective-permute-done.9.x2 = bf16[512,512]{1,0:T(8,128)(2,1)S(1)} collective-permute-done((bf16[512,512]{1,0:T(8,128)(2,1)S(1)}, bf16[512,512]{1,0:T(8,128)(2,1)S(1)}, u32[]{:S(2)}, u32[]{:S(2)}) %collective-permute-start.9) | collective-permute-done | bytes 524320 | tf_op jit(solution)/shard_map/ppermute | solution.py:493
  64.4 10.0 %collective-permute-done.1.x2 = bf16[512,512]{1,0:T(8,128)(2,1)} collective-permute-done((bf16[512,512]{1,0:T(8,128)(2,1)S(1)}, bf16[512,512]{1,0:T(8,128)(2,1)}, u32[]{:S(2)}, u32[]{:S(2)}) %collective-permute-start.1) | collective-permute-done | bytes 524320 | tf_op jit(solution)/shard_map/ppermute | solution.py:493
  78.9 5.4 %hidden.3.h0 = bf16[512,384]{1,0:T(8,128)(2,1)} custom-call(s32[1]{0:T(128)} %bitcast.2.pos_ref, bf16[1024,512]{1,0:T(8,128)(2,1)} %bitcast.33, bf16[1024,512]{1,0:T(8,128)(2,1)} %copy-done.1, bf16[512,512]{1,0:T(8,128)(2,1)} %copy-done.11, bf16[512,512]{1,0:T(8,128)(2,1)} %collective-permute-done.10.x3, bf16[1,352,2048]{2,1,0:T(8,128)(2,1)} %bitcast.16, ...), custom_call_target="tpu_custom_call" | custom-call | flops 1476395008 | bytes 6000000 | tf_op jit(solution)/shard_map/hidden/pallas_call | solution.py:247
  85.5 5.5 %hidden.2.h0.refs_4_ = bf16[512,384]{1,0:T(8,128)(2,1)} custom-call(s32[1]{0:T(128)} %bitcast.2.pos_ref, bf16[1024,512]{1,0:T(8,128)(2,1)} %bitcast.34, bf16[1024,512]{1,0:T(8,128)(2,1)} %copy-done.1, bf16[512,512]{1,0:T(8,128)(2,1)} %collective-permute-done.1.x2, bf16[512,512]{1,0:T(8,128)(2,1)} %collective-permute-done.2.x3, ...), custom_call_target="tpu_custom_call" | custom-call | flops 1476395008 | bytes 6000000 | tf_op jit(solution)/shard_map/hidden/pallas_call | solution.py:247
  97.6 14.9 %collective-permute-done.7.w2 = bf16[352,512]{1,0:T(8,128)(2,1)S(1)} collective-permute-done((bf16[352,512]{1,0:T(8,128)(2,1)S(1)}, bf16[352,512]{1,0:T(8,128)(2,1)S(1)}, u32[]{:S(2)}, u32[]{:S(2)}) %collective-permute-start.7) | collective-permute-done | bytes 360480 | tf_op jit(solution)/shard_map/ppermute | solution.py:479
  113.9 3.9 %down.2.rest_0_ = bf16[1024,512]{1,0:T(8,128)(2,1)} custom-call(s32[1]{0:T(128)} %bitcast.2.pos_ref, bf16[512,384]{1,0:T(8,128)(2,1)} %hidden.3.h0, bf16[512,384]{1,0:T(8,128)(2,1)} %copy-done.17, bf16[512,384]{1,0:T(8,128)(2,1)} %collective-permute-done.12.h2, bf16[512,384]{1,0:T(8,128)(2,1)} %copy-done.18, bf16[1,352,2048]{2,1,0:T(8,128)(2,1)} %w0.3, ...), custom_call_target="tpu_custom_call" | custom-call | flops 738197504 | bytes 4000000 | tf_op jit(solution)/shard_map/down/pallas_call | solution.py:279
  119.3 3.9 %down.3.refs_4_ = bf16[1024,512]{1,0:T(8,128)(2,1)} custom-call(s32[1]{0:T(128)} %bitcast.2.pos_ref, bf16[512,384]{1,0:T(8,128)(2,1)} %hidden.2.h0.refs_4_, bf16[512,384]{1,0:T(8,128)(2,1)} %copy-done.14, bf16[512,384]{1,0:T(8,128)(2,1)} %copy-done.16, bf16[512,384]{1,0:T(8,128)(2,1)} %copy-done.15, ...), custom_call_target="tpu_custom_call", output_to_operand_aliasing={{}: (9, {})} | custom-call | flops 738197504 | bytes 4000000 | tf_op jit(solution)/shard_map/down/pallas_call | solution.py:279
  123.2 6.1 %all-to-all-start.1 = ((bf16[64,16,512]{2,1,0:T(8,128)(2,1)}), bf16[64,16,512]{2,1,0:T(8,128)(2,1)S(1)}, u32[]{:S(2)}, u32[]{:S(2)}) async-start(bf16[64,16,512]{2,1,0:T(8,128)(2,1)} %bitcast.35), calls=%async_computation.1 | async-start | bytes 2097152 | tf_op jit(solution)/shard_map/all_to_all | solution.py:512
  136.8 5.2 %collective-permute-done.17.refs_1_ = bf16[4,32,640]{2,1,0:T(8,128)(2,1)S(1)} collective-permute-done((bf16[4,32,640]{2,1,0:T(8,128)(2,1)}, bf16[4,32,640]{2,1,0:T(8,128)(2,1)S(1)}, u32[]{:S(2)}, u32[]{:S(2)}) %collective-permute-start.17) | collective-permute-done | bytes 163872 | tf_op jit(solution)/shard_map/ppermute | solution.py:467
  141.9 14.5 %collective-permute-done.18.refs_2_ = bf16[4,32,640]{2,1,0:T(8,128)(2,1)S(1)} collective-permute-done((bf16[4,32,640]{2,1,0:T(8,128)(2,1)}, bf16[4,32,640]{2,1,0:T(8,128)(2,1)S(1)}, u32[]{:S(2)}, u32[]{:S(2)}) %collective-permute-start.18) | collective-permute-done | bytes 163872 | tf_op jit(solution)/shard_map/ppermute | solution.py:467
  156.5 5.9 %collective-permute-done.19.refs_3_ = bf16[4,32,640]{2,1,0:T(8,128)(2,1)S(1)} collective-permute-done((bf16[4,32,640]{2,1,0:T(8,128)(2,1)}, bf16[4,32,640]{2,1,0:T(8,128)(2,1)S(1)}, u32[]{:S(2)}, u32[]{:S(2)}) %collective-permute-start.19) | collective-permute-done | bytes 163872 | tf_op jit(solution)/shard_map/ppermute | solution.py:467
  165.1 4.3 %collective-permute-start.23 = (bf16[128,256]{1,0:T(8,128)(2,1)}, bf16[128,256]{1,0:T(8,128)(2,1)S(1)}, u32[]{:S(2)}, u32[]{:S(2)}) collective-permute-start(bf16[128,256]{1,0:T(8,128)(2,1)} %get-tuple-element.27), channel_id=1, source_target_pairs={{0,0},{1,64},{2,128},{3,192},{4,4},{5,68},{6,132},{7,196},{8,8},{9... | collective-permute-start | bytes 196616 | tf_op jit(solution)/shard_map/ppermute | solution.py:474
  179.1 3.5 %collective-permute-done.26.refs_7_ = bf16[128,256]{1,0:T(8,128)(2,1)S(1)} collective-permute-done((bf16[128,256]{1,0:T(8,128)(2,1)}, bf16[128,256]{1,0:T(8,128)(2,1)S(1)}, u32[]{:S(2)}, u32[]{:S(2)}) %collective-permute-start.26) | collective-permute-done | bytes 65568 | tf_op jit(solution)/shard_map/ppermute | solution.py:474
  187.5 3.5 %collective-permute-start.28 = (bf16[4,2,64,640]{3,2,1,0:T(8,128)(2,1)}, bf16[4,2,64,640]{3,2,1,0:T(8,128)(2,1)S(1)}, u32[]{:S(2)}, u32[]{:S(2)}) collective-permute-start(bf16[4,2,64,640]{3,2,1,0:T(8,128)(2,1)} %bitcast.37), channel_id=1, source_target_pairs={{0,16},{4,20},{8,24},{12,28},{16,0},{20,4},{24,8},{28,12},{32,48},... | collective-permute-start | bytes 1966088 | tf_op jit(solution)/shard_map/ppermute | solution.py:486
  197.2 9.9 %collective-permute-done.15.t2 = bf16[128,2048]{1,0:T(8,128)(2,1)S(1)} collective-permute-done((bf16[128,2048]{1,0:T(8,128)(2,1)S(1)}, bf16[128,2048]{1,0:T(8,128)(2,1)S(1)}, u32[]{:S(2)}, u32[]{:S(2)}) %collective-permute-start.15) | collective-permute-done | bytes 524320 | tf_op jit(solution)/shard_map/ppermute | solution.py:489
  207.1 13.2 %collective-permute-done.16.t3 = bf16[128,2048]{1,0:T(8,128)(2,1)S(1)} collective-permute-done((bf16[128,2048]{1,0:T(8,128)(2,1)S(1)}, bf16[128,2048]{1,0:T(8,128)(2,1)S(1)}, u32[]{:S(2)}, u32[]{:S(2)}) %collective-permute-start.16) | collective-permute-done | bytes 524320 | tf_op jit(solution)/shard_map/ppermute | solution.py:489
  220.3 17.9 %collective-permute-done.28.refs_2_ = bf16[4,2,64,640]{3,2,1,0:T(8,128)(2,1)S(1)} collective-permute-done((bf16[4,2,64,640]{3,2,1,0:T(8,128)(2,1)}, bf16[4,2,64,640]{3,2,1,0:T(8,128)(2,1)S(1)}, u32[]{:S(2)}, u32[]{:S(2)}) %collective-permute-start.28) | collective-permute-done | bytes 655392 | tf_op jit(solution)/shard_map/ppermute | solution.py:486
  238.3 11.0 %collective-permute-done.29.refs_3_ = bf16[4,2,64,640]{3,2,1,0:T(8,128)(2,1)S(1)} collective-permute-done((bf16[4,2,64,640]{3,2,1,0:T(8,128)(2,1)}, bf16[4,2,64,640]{3,2,1,0:T(8,128)(2,1)S(1)}, u32[]{:S(2)}, u32[]{:S(2)}) %collective-permute-start.29) | collective-permute-done | bytes 655392 | tf_op jit(solution)/shard_map/ppermute | solution.py:486
  250.1 4.9 %shared_hidden.1.h0 = bf16[512,256]{1,0:T(8,128)(2,1)} custom-call(s32[4]{0:T(128)} %pad_add_fusion.place_ref, bf16[128,2048]{1,0:T(8,128)(2,1)} %t0.1, bf16[128,2048]{1,0:T(8,128)(2,1)} %collective-permute-done.14.t1, bf16[128,2048]{1,0:T(8,128)(2,1)} %copy-done.12, bf16[128,2048]{1,0:T(8,128)(2,1)} %copy-done.13, bf16[4,2,64,640]{3,2,1,0:T(8,128)(2,1)} %bitcast.39, ...), custom_call_target="tpu_custom_call" | custom-call | flops 805306368 | bytes 5000000 | tf_op jit(solution)/shard_map/shared_hidden/pallas_call | solution.py:330
  258.4 5.6 %collective-permute-done.31.h2 = bf16[512,256]{1,0:T(8,128)(2,1)S(1)} collective-permute-done((bf16[512,256]{1,0:T(8,128)(2,1)}, bf16[512,256]{1,0:T(8,128)(2,1)S(1)}, u32[]{:S(2)}, u32[]{:S(2)}) %collective-permute-start.31) | collective-permute-done | bytes 262176 | tf_op jit(solution)/shard_map/ppermute | solution.py:504
  267.0 3.8 %shared_down.1 = (bf16[128,512]{1,0:T(8,128)(2,1)}, bf16[128,512]{1,0:T(8,128)(2,1)}, bf16[128,512]{1,0:T(8,128)(2,1)}, bf16[128,512]{1,0:T(8,128)(2,1)}) custom-call(s32[4]{0:T(128)} %pad_add_fusion.place_ref, bf16[512,256]{1,0:T(8,128)(2,1)} %shared_hidden.1.h0, bf16[512,256]{1,0:T(8,128)(2,1)} %copy-done.20, bf16[512,256]{1,0:T(8,128)(2,1)} %copy-done.19, ...), custom_call_target="tpu_custom_call" | custom-call | flops 536870912 | bytes 4000000 | tf_op jit(solution)/shard_map/shared_down/pallas_call | solution.py:366
  279.4 3.2 %collective-permute-done.35.s3 = bf16[128,512]{1,0:T(8,128)(2,1)S(1)} collective-permute-done((bf16[128,512]{1,0:T(8,128)(2,1)}, bf16[128,512]{1,0:T(8,128)(2,1)S(1)}, u32[]{:S(2)}, u32[]{:S(2)}) %collective-permute-start.35) | collective-permute-done | bytes 131104 | tf_op jit(solution)/shard_map/ppermute | solution.py:516
  (138 shorter events, 71.5 us)
Async XLA Ops:
  45.2 32.7 %collective-permute-start = (bf16[1024,512]{1,0:T(8,128)(2,1)S(1)}, bf16[1024,512]{1,0:T(8,128)(2,1)S(1)}, u32[]{:S(2)}, u32[]{:S(2)}) collective-permute-start(bf16[1024,512]{1,0:T(8,128)(2,1)S(1)} %bitcast.32), channel_id=1, source_target_pairs={{0,1},{1,0},{2,3},{3,2},{4,5},{5,4},{6,7},{7,6},{8,9},{9,8},{10,11... | collective-permute-start | bytes 3145736 | tf_op jit(solution)/shard_map/ppermute | solution.py:494
  49.5 13.6 %collective-permute-start.9 = (bf16[512,512]{1,0:T(8,128)(2,1)S(1)}, bf16[512,512]{1,0:T(8,128)(2,1)S(1)}, u32[]{:S(2)}, u32[]{:S(2)}) collective-permute-start(bf16[512,512]{1,0:T(8,128)(2,1)S(1)} %bitcast.44), channel_id=1, source_target_pairs={{0,2},{2,0},{1,3},{3,1},{4,6},{6,4},{5,7},{7,5},{8,10},{10,8},{9,1... | collective-permute-start | bytes 1572872 | tf_op jit(solution)/shard_map/ppermute | solution.py:493
  50.0 24.4 %collective-permute-start.1 = (bf16[512,512]{1,0:T(8,128)(2,1)S(1)}, bf16[512,512]{1,0:T(8,128)(2,1)}, u32[]{:S(2)}, u32[]{:S(2)}) collective-permute-start(bf16[512,512]{1,0:T(8,128)(2,1)S(1)} %bitcast.43), channel_id=1, source_target_pairs={{0,2},{2,0},{1,3},{3,1},{4,6},{6,4},{5,7},{7,5},{8,10},{10,8},{9,1... | collective-permute-start | bytes 1572872 | tf_op jit(solution)/shard_map/ppermute | solution.py:493
  63.0 14.9 %collective-permute-start.10 = (bf16[512,512]{1,0:T(8,128)(2,1)S(1)}, bf16[512,512]{1,0:T(8,128)(2,1)}, u32[]{:S(2)}, u32[]{:S(2)}) collective-permute-start(bf16[512,512]{1,0:T(8,128)(2,1)S(1)} %collective-permute-done.9.x2), channel_id=1, source_target_pairs={{0,1},{1,0},{2,3},{3,2},{4,5},{5,4},{6,7},{7,6},{8,9},{9,8},{10,11... | collective-permute-start | bytes 1572872 | tf_op jit(solution)/shard_map/ppermute | solution.py:497
  74.4 11.2 %collective-permute-start.2 = (bf16[512,512]{1,0:T(8,128)(2,1)}, bf16[512,512]{1,0:T(8,128)(2,1)}, u32[]{:S(2)}, u32[]{:S(2)}) collective-permute-start(bf16[512,512]{1,0:T(8,128)(2,1)} %collective-permute-done.1.x2), channel_id=1, source_target_pairs={{0,1},{1,0},{2,3},{3,2},{4,5},{5,4},{6,7},{7,6},{8,9},{9,8},{10,11... | collective-permute-start | bytes 1572872 | tf_op jit(solution)/shard_map/ppermute | solution.py:497
  77.5 19.9 %collective-permute-start.6 = (bf16[352,512]{1,0:T(8,128)(2,1)}, bf16[352,512]{1,0:T(8,128)(2,1)S(1)}, u32[]{:S(2)}, u32[]{:S(2)}) collective-permute-start(bf16[352,512]{1,0:T(8,128)(2,1)} %get-tuple-element.20), channel_id=1, source_target_pairs={{0,2},{2,0},{1,3},{3,1},{4,6},{6,4},{5,7},{7,5},{8,10},{10,8},{9,1... | collective-permute-start | bytes 1081352 | tf_op jit(solution)/shard_map/ppermute | solution.py:479
  84.4 11.7 %collective-permute-start.11 = (bf16[512,384]{1,0:T(8,128)(2,1)}, bf16[512,384]{1,0:T(8,128)(2,1)S(1)}, u32[]{:S(2)}, u32[]{:S(2)}) collective-permute-start(bf16[512,384]{1,0:T(8,128)(2,1)} %hidden.3.h0), channel_id=1, source_target_pairs={{0,2},{2,0},{1,3},{3,1},{4,6},{6,4},{5,7},{7,5},{8,10},{10,8},{9,1... | collective-permute-start | bytes 1179656 | tf_op jit(solution)/shard_map/ppermute | solution.py:499
  91.0 21.7 %collective-permute-start.3 = (bf16[512,384]{1,0:T(8,128)(2,1)}, bf16[512,384]{1,0:T(8,128)(2,1)S(1)}, u32[]{:S(2)}, u32[]{:S(2)}) collective-permute-start(bf16[512,384]{1,0:T(8,128)(2,1)} %hidden.2.h0.refs_4_), channel_id=1, source_target_pairs={{0,2},{2,0},{1,3},{3,1},{4,6},{6,4},{5,7},{7,5},{8,10},{10,8},{9,1... | collective-permute-start | bytes 1179656 | tf_op jit(solution)/shard_map/ppermute | solution.py:499
  91.4 21.0 %collective-permute-start.7 = (bf16[352,512]{1,0:T(8,128)(2,1)S(1)}, bf16[352,512]{1,0:T(8,128)(2,1)S(1)}, u32[]{:S(2)}, u32[]{:S(2)}) collective-permute-start(bf16[352,512]{1,0:T(8,128)(2,1)S(1)} %copy-done.35), channel_id=1, source_target_pairs={{0,3},{3,0},{1,2},{2,1},{4,7},{7,4},{5,6},{6,5},{8,11},{11,8},{9,1... | collective-permute-start | bytes 1081352 | tf_op jit(solution)/shard_map/ppermute | solution.py:479
  93.2 19.7 %collective-permute-start.13 = (bf16[512,384]{1,0:T(8,128)(2,1)S(1)}, bf16[512,384]{1,0:T(8,128)(2,1)S(1)}, u32[]{:S(2)}, u32[]{:S(2)}) collective-permute-start(bf16[512,384]{1,0:T(8,128)(2,1)S(1)} %copy-done.7), channel_id=1, source_target_pairs={{0,1},{1,0},{2,3},{3,2},{4,5},{5,4},{6,7},{7,6},{8,9},{9,8},{10,11... | collective-permute-start | bytes 1179656 | tf_op jit(solution)/shard_map/ppermute | solution.py:500
  96.1 17.6 %collective-permute-start.12 = (bf16[512,384]{1,0:T(8,128)(2,1)S(1)}, bf16[512,384]{1,0:T(8,128)(2,1)}, u32[]{:S(2)}, u32[]{:S(2)}) collective-permute-start(bf16[512,384]{1,0:T(8,128)(2,1)S(1)} %collective-permute-done.11.h1), channel_id=1, source_target_pairs={{0,1},{1,0},{2,3},{3,2},{4,5},{5,4},{6,7},{7,6},{8,9},{9,8},{10,11... | collective-permute-start | bytes 1179656 | tf_op jit(solution)/shard_map/ppermute | solution.py:509
  97.5 15.5 %collective-permute-start.8 = (bf16[352,512]{1,0:T(8,128)(2,1)}, bf16[352,512]{1,0:T(8,128)(2,1)S(1)}, u32[]{:S(2)}, u32[]{:S(2)}) collective-permute-start(bf16[352,512]{1,0:T(8,128)(2,1)} %get-tuple-element.22), channel_id=1, source_target_pairs={{0,1},{1,0},{2,3},{3,2},{4,5},{5,4},{6,7},{7,6},{8,9},{9,8},{10,11... | collective-permute-start | bytes 1081352 | tf_op jit(solution)/shard_map/ppermute | solution.py:479
  123.2 159.4 %all-to-all-start.1 = ((bf16[64,16,512]{2,1,0:T(8,128)(2,1)}), bf16[64,16,512]{2,1,0:T(8,128)(2,1)S(1)}, u32[]{:S(2)}, u32[]{:S(2)}) async-start(bf16[64,16,512]{2,1,0:T(8,128)(2,1)} %bitcast.35), calls=%async_computation.1 | async-start | bytes 2097152 | tf_op jit(solution)/shard_map/all_to_all | solution.py:512
  129.3 65.1 %collective-permute-start.14 = (bf16[128,2048]{1,0:T(8,128)(2,1)S(1)}, bf16[128,2048]{1,0:T(8,128)(2,1)}, u32[]{:S(2)}, u32[]{:S(2)}) collective-permute-start(bf16[128,2048]{1,0:T(8,128)(2,1)S(1)} %copy-done.6), channel_id=1, source_target_pairs={{0,64},{4,68},{8,72},{12,76},{16,80},{20,84},{24,88},{28,92},{32,9... | collective-permute-start | bytes 1572872 | tf_op jit(solution)/shard_map/ppermute | solution.py:489
  132.0 10.0 %collective-permute-start.17 = (bf16[4,32,640]{2,1,0:T(8,128)(2,1)}, bf16[4,32,640]{2,1,0:T(8,128)(2,1)S(1)}, u32[]{:S(2)}, u32[]{:S(2)}) collective-permute-start(bf16[4,32,640]{2,1,0:T(8,128)(2,1)} %pack.1.refs_0_), channel_id=1, source_target_pairs={{0,32},{4,36},{8,40},{12,44},{16,48},{20,52},{24,56},{28,60},{32,0... | collective-permute-start | bytes 491528 | tf_op jit(solution)/shard_map/ppermute | solution.py:467
  134.7 21.8 %collective-permute-start.18 = (bf16[4,32,640]{2,1,0:T(8,128)(2,1)}, bf16[4,32,640]{2,1,0:T(8,128)(2,1)S(1)}, u32[]{:S(2)}, u32[]{:S(2)}) collective-permute-start(bf16[4,32,640]{2,1,0:T(8,128)(2,1)} %pack.1.refs_0_), channel_id=1, source_target_pairs={{0,4},{4,0},{8,12},{12,8},{16,20},{20,16},{24,28},{28,24},{32,36},... | collective-permute-start | bytes 491528 | tf_op jit(solution)/shard_map/ppermute | solution.py:467
  135.9 26.5 %collective-permute-start.19 = (bf16[4,32,640]{2,1,0:T(8,128)(2,1)}, bf16[4,32,640]{2,1,0:T(8,128)(2,1)S(1)}, u32[]{:S(2)}, u32[]{:S(2)}) collective-permute-start(bf16[4,32,640]{2,1,0:T(8,128)(2,1)} %pack.1.refs_0_), channel_id=1, source_target_pairs={{0,36},{4,32},{8,44},{12,40},{16,52},{20,48},{24,60},{28,56},{32,4... | collective-permute-start | bytes 491528 | tf_op jit(solution)/shard_map/ppermute | solution.py:467
  185.4 34.9 %collective-permute-start.27 = (bf16[4,2,64,640]{3,2,1,0:T(8,128)(2,1)}, bf16[4,2,64,640]{3,2,1,0:T(8,128)(2,1)S(1)}, u32[]{:S(2)}, u32[]{:S(2)}) collective-permute-start(bf16[4,2,64,640]{3,2,1,0:T(8,128)(2,1)} %bitcast.36), channel_id=1, source_target_pairs={{0,8},{4,12},{8,16},{12,20},{16,24},{20,28},{24,0},{28,4},{32,40},... | collective-permute-start | bytes 1966088 | tf_op jit(solution)/shard_map/ppermute | solution.py:486
  187.5 50.8 %collective-permute-start.28 = (bf16[4,2,64,640]{3,2,1,0:T(8,128)(2,1)}, bf16[4,2,64,640]{3,2,1,0:T(8,128)(2,1)S(1)}, u32[]{:S(2)}, u32[]{:S(2)}) collective-permute-start(bf16[4,2,64,640]{3,2,1,0:T(8,128)(2,1)} %bitcast.37), channel_id=1, source_target_pairs={{0,16},{4,20},{8,24},{12,28},{16,0},{20,4},{24,8},{28,12},{32,48},... | collective-permute-start | bytes 1966088 | tf_op jit(solution)/shard_map/ppermute | solution.py:486
  190.9 58.3 %collective-permute-start.29 = (bf16[4,2,64,640]{3,2,1,0:T(8,128)(2,1)}, bf16[4,2,64,640]{3,2,1,0:T(8,128)(2,1)S(1)}, u32[]{:S(2)}, u32[]{:S(2)}) collective-permute-start(bf16[4,2,64,640]{3,2,1,0:T(8,128)(2,1)} %bitcast.38), channel_id=1, source_target_pairs={{0,24},{4,28},{8,0},{12,4},{16,8},{20,12},{24,16},{28,20},{32,56},... | collective-permute-start | bytes 1966088 | tf_op jit(solution)/shard_map/ppermute | solution.py:486
  193.8 13.3 %collective-permute-start.15 = (bf16[128,2048]{1,0:T(8,128)(2,1)S(1)}, bf16[128,2048]{1,0:T(8,128)(2,1)S(1)}, u32[]{:S(2)}, u32[]{:S(2)}) collective-permute-start(bf16[128,2048]{1,0:T(8,128)(2,1)S(1)} %copy-done.6), channel_id=1, source_target_pairs={{0,128},{4,132},{8,136},{12,140},{16,144},{20,148},{24,152},{28,15... | collective-permute-start | bytes 1572872 | tf_op jit(solution)/shard_map/ppermute | solution.py:489
  194.4 25.9 %collective-permute-start.16 = (bf16[128,2048]{1,0:T(8,128)(2,1)S(1)}, bf16[128,2048]{1,0:T(8,128)(2,1)S(1)}, u32[]{:S(2)}, u32[]{:S(2)}) collective-permute-start(bf16[128,2048]{1,0:T(8,128)(2,1)S(1)} %copy-done.6), channel_id=1, source_target_pairs={{0,192},{4,196},{8,200},{12,204},{16,208},{20,212},{24,216},{28,22... | collective-permute-start | bytes 1572872 | tf_op jit(solution)/shard_map/ppermute | solution.py:489
  255.0 9.0 %collective-permute-start.31 = (bf16[512,256]{1,0:T(8,128)(2,1)}, bf16[512,256]{1,0:T(8,128)(2,1)S(1)}, u32[]{:S(2)}, u32[]{:S(2)}) collective-permute-start(bf16[512,256]{1,0:T(8,128)(2,1)} %shared_hidden.1.h0), channel_id=1, source_target_pairs={{0,2},{2,0},{1,3},{3,1},{4,6},{6,4},{5,7},{7,5},{8,10},{10,8},{9,1... | collective-permute-start | bytes 786440 | tf_op jit(solution)/shard_map/ppermute | solution.py:504
  273.2 9.4 %collective-permute-start.35 = (bf16[128,512]{1,0:T(8,128)(2,1)}, bf16[128,512]{1,0:T(8,128)(2,1)S(1)}, u32[]{:S(2)}, u32[]{:S(2)}) collective-permute-start(bf16[128,512]{1,0:T(8,128)(2,1)} %get-tuple-element.34), channel_id=1, source_target_pairs={{0,64},{4,68},{8,72},{12,76},{16,80},{20,84},{24,88},{28,92},{32,9... | collective-permute-start | bytes 393224 | tf_op jit(solution)/shard_map/ppermute | solution.py:516
  (49 other events, 351.4 us)
